TPU v7x, 32 devices: a whole 2x2x4 slice. The times are simulated.
32 devices in a mesh: rep: 1, r: 8 (over y, z), s: 4 (over x, core).
Axes of the slice: x: 2, y: 2, z: 4, core: 2. Of those that a mesh axis runs over, the one named last changes fastest.
Arguments:
- x: bfloat16 [32, 4096, 640], P(('rep', 'r', 's'))
- dy: bfloat16 [32, 4096, 640], P(('rep', 'r', 's'))
- w_gate: bfloat16 [2, 640, 2048], P(None, 's')
- w_up: bfloat16 [2, 640, 2048], P(None, 's')
- w_down: bfloat16 [2, 2048, 640], P(None, 's')
Outputs:
- output 1: bfloat16 [32, 4096, 640], P(('rep', 'r', 's'))
- output 2: bfloat16 [2, 640, 2048], P('rep', 's')
- output 3: bfloat16 [2, 640, 2048], P('rep', 's')
- output 4: bfloat16 [2, 2048, 640], P('rep', 's')
All inputs are finite; a program needn't handle non-finite values.
Results may differ from a plain program's by a relative error of at most 0.018.
Values are sent between devices in bfloat16 or wider.
A program may use at most 2 GiB of HBM per device.

v0:
```python
import jax
import jax.numpy as jnp
from jax import lax
from jax.sharding import PartitionSpec as P

NAMES = ("w_gate", "w_up", "w_down")


def matmul(a, w):
    return jnp.dot(a, w, preferred_element_type=jnp.float32).astype(jnp.bfloat16)


def normed(h):
    wide = h.astype(jnp.float32)
    scale = lax.rsqrt(jnp.mean(wide**2, -1, keepdims=True) + 1e-6)
    return (wide * scale).astype(jnp.bfloat16)


def layer(h, w):
    a = normed(h)
    gate = jnp.dot(a, w["w_gate"], preferred_element_type=jnp.float32)
    up = jnp.dot(a, w["w_up"], preferred_element_type=jnp.float32)
    return h + matmul((jax.nn.silu(gate) * up).astype(jnp.bfloat16), w["w_down"])


def solution(mesh):
    def fetched(weights, number):
        return {name: lax.all_gather(w[number], "s", axis=0, tiled=True) for name, w in zip(NAMES, weights, strict=True)}

    def summed(term):
        return lax.psum(lax.psum_scatter(term, "s", scatter_dimension=0, tiled=True), "r")

    def step(x, dy, *weights):
        layers = weights[0].shape[0]
        h, inputs = x[0], []
        for number in range(layers):
            inputs.append(h)
            h = layer(h, fetched(weights, number))
        by_h, mine = dy[0], [None] * layers
        for number in reversed(range(layers)):
            _, back = jax.vjp(lambda w, h: layer(h, w), fetched(weights, number), inputs[number])
            by_w, by_h = back(by_h)
            mine[number] = [summed(by_w[name]) for name in NAMES]
        return (by_h[None], *(jnp.stack([mine[number][i] for number in range(layers)]) for i in range(3)))

    states, cut = P(("rep", "r", "s"), None, None), P(None, "s", None)
    return jax.shard_map(
        step,
        mesh=mesh,
        in_specs=(states, states) + (cut,) * 3,
        out_specs=(states,) + (P("rep", "s", None),) * 3,
        check_vma=False,
    )
```

profile of v0, /device:TPU:0, one launch (start us, length us, event | category | flops | bytes accessed | tf_op | source)
XLA Modules:
  0.0 694.1 jit_solution(12911573054573444433)
XLA Ops:
  9.8 2.5 fusion.79
  12.3 2.5 fusion.78
  16.7 7.9 %copy.10 = bf16[1,4096,640]{1,2,0:T(8,128)(2,1)} copy(bf16[1,4096,640]{2,1,0:T(8,128)(2,1)} %param.5) | data formatting | bytes 10485760 | tf_op args[0]
  24.5 3.6 fusion.15
  28.8 8.0 %copy.9 = bf16[1,4096,640]{1,2,0:T(8,128)(2,1)} copy(bf16[1,4096,640]{2,1,0:T(8,128)(2,1)} %param.6) | data formatting | bytes 10485760 | tf_op args[1]
  38.1 21.8 %fusion.43 = f32[4096,2048]{1,0:T(8,128)} fusion(bf16[1,4096,640]{1,2,0:T(8,128)(2,1)} %copy.10, f32[4096]{0:T(1024)S(1)} %fusion.71, bf16[1,640,2048]{2,1,0:T(8,128)(2,1)} %all-gather.13.cloned.1.call-done), kind=kOutput, calls=%fused_computation.61 | convolution fusion | flops 10745282560 | bytes 41435136 | tf_op jit(solution)/shard_map/dot_general | solution.py:21
  59.9 5.0 all-gather.15.cloned.1.call-done
  64.9 33.7 %multiply_convert_fusion.1 = (bf16[4096,2048]{1,0:T(8,128)(2,1)}, f32[4096,2048]{1,0:T(8,128)}) fusion(f32[4096,2048]{1,0:T(8,128)} %fusion.43, bf16[1,640,2048]{2,1,0:T(8,128)(2,1)} %all-gather.15.cloned.1.call-done, bf16[1,4096,640]{1,2,0:T(8,128)(2,1)} %copy.10, f32[4096]{0:T(1024)S(1)} %fusion.71), kind=kOutput, calls=%fused_computation.13 | convolution fusion | flops 10795614208 | bytes 91766784 | tf_op jit(solution)/shard_map/dot_general | solution.py:22
  98.6 18.5 %fusion.18 = (f32[4096]{0:T(1024)S(1)}, bf16[4096,640]{0,1:T(8,128)(2,1)}) fusion(bf16[4096,2048]{1,0:T(8,128)(2,1)} %get-tuple-element.20, bf16[1,2048,640]{2,1,0:T(8,128)(2,1)} %all-gather.17.cloned.1.call-done, bf16[1,4096,640]{1,2,0:T(8,128)(2,1)} %copy.10), kind=kOutput, calls=%fused_computation.40 | convolution fusion | flops 10750521344 | bytes 29900800 | tf_op jit(solution)/shard_map/dot_general | solution.py:10
  118.4 20.1 %convolution_convert_fusion.1 = bf16[4096,2048]{1,0:T(8,128)(2,1)} fusion(bf16[1,4096,640]{2,1,0:T(8,128)(2,1)} %param.6, bf16[1,2048,640]{2,1,0:T(8,128)(2,1)} %all-gather.21.cloned.1.call-done), kind=kOutput, calls=%fused_computation.30 | convolution fusion | flops 10745806848 | bytes 24641536 | tf_op jit(solution)/shard_map/transpose(jvp())/dot_general | solution.py:10
  138.5 7.1 %all-gather.23.cloned.1.call-done = bf16[1,640,2048]{2,1,0:T(8,128)(2,1)} async-done(((bf16[1,160,2048]{2,1,0:T(8,128)(2,1)}), bf16[1,640,2048]{2,1,0:T(8,128)(2,1)}) %all-gather.23.cloned.1.call-update) | async-done | bytes 2621456 | tf_op jit(solution)/shard_map/all_gather | solution.py:28
  145.6 21.8 %fusion.34 = f32[4096,2048]{1,0:T(8,128)} fusion(bf16[4096,640]{0,1:T(8,128)(2,1)} %get-tuple-element.23, f32[4096]{0:T(1024)S(1)} %fusion.72, bf16[1,640,2048]{2,1,0:T(8,128)(2,1)} %all-gather.23.cloned.1.call-done), kind=kOutput, calls=%fused_computation.57 | convolution fusion | flops 10745282560 | bytes 41435136 | tf_op jit(solution)/shard_map/jvp()/dot_general | solution.py:22
  167.3 5.5 all-gather.19.cloned.1.call-done
  172.8 44.7 %fusion.1 = (bf16[4096,2048]{1,0:T(8,128)(2,1)}, f32[4096,2048]{1,0:T(8,128)}) fusion(f32[4096,2048]{1,0:T(8,128)} %fusion.34, bf16[4096,2048]{1,0:T(8,128)(2,1)} %convolution_convert_fusion.1, bf16[1,640,2048]{2,1,0:T(8,128)(2,1)} %all-gather.19.cloned.1.call-done, bf16[4096,640]{0,1:T(8,128)(2,1)} %get-tuple-element.23, f32[4096]{0:T(1024)S(1)} %fusion.72), kind=kOutput, calls=%fused_computation.7 | convolution fusion | flops 10845945856 | bytes 108544000 | tf_op jit(solution)/shard_map/jvp()/dot_general | solution.py:21
  217.5 17.0 %convolution_convert_fusion.4 = bf16[4096,640]{0,1:T(8,128)(2,1)} fusion(bf16[4096,2048]{1,0:T(8,128)(2,1)} %get-tuple-element.24, bf16[1,640,2048]{2,1,0:T(8,128)(2,1)} %all-gather.19.cloned.1.call-done), kind=kOutput, calls=%fused_computation.47 | convolution fusion | flops 10737418240 | bytes 24641536 | tf_op jit(solution)/shard_map/transpose(jvp())/dot_general | solution.py:21
  234.5 25.3 %fusion.20 = (f32[4096]{0:T(1024)S(1)}, bf16[4096,640]{0,1:T(8,128)(2,1)}) fusion(bf16[4096,640]{0,1:T(8,128)(2,1)} %get-tuple-element.23, bf16[4096,640]{0,1:T(8,128)(2,1)} %convolution_convert_fusion.4, bf16[1,640,2048]{2,1,0:T(8,128)(2,1)S(1)} %copy-done.10, bf16[4096,2048]{1,0:T(8,128)(2,1)} %convolution_convert_fusion.1, ...), kind=kOutput, calls=%fused_computation.42 | convolution fusion | flops 10803474432 | bytes 68698112 | tf_op jit(solution)/shard_map/transpose(jvp())/dot_general | solution.py:22
  259.9 11.9 %fusion.28 = bf16[4096,640]{0,1:T(8,128)(2,1)} fusion(bf16[4096,640]{0,1:T(8,128)(2,1)} %get-tuple-element.23, bf16[4096,640]{0,1:T(8,128)(2,1)} %get-tuple-element.27, bf16[1,4096,640]{1,2,0:T(8,128)(2,1)} %copy.9, f32[4096]{0:T(1024)S(1)} %multiply_multiply_fusion.1, f32[4096]{0:T(1024)S(1)} %fusion.72), kind=kLoop, calls=%fused_computation.53 | loop fusion | flops 18350080 | bytes 21004288 | tf_op jit(solution)/shard_map/transpose(jvp())/add_any | solution.py:14
  271.8 19.8 %convolution_convert_fusion.5 = bf16[2048,640]{1,0:T(8,128)(2,1)} fusion(bf16[4096,2048]{1,0:T(8,128)(2,1)} %get-tuple-element.20, bf16[4096,640]{0,1:T(8,128)(2,1)} %fusion.28), kind=kOutput, calls=%fused_computation.67 | convolution fusion | flops 10738728960 | bytes 24641536 | tf_op jit(solution)/shard_map/transpose(jvp())/dot_general | solution.py:10
  291.7 27.2 %fusion.51 = bf16[2048,640]{1,0:T(8,128)(2,1)} fusion(bf16[1,4096,640]{2,1,0:T(8,128)(2,1)} %param.6, f32[4096,2048]{1,0:T(8,128)} %fusion.34, f32[4096,2048]{1,0:T(8,128)} %get-tuple-element.25), kind=kOutput, calls=%fused_computation.64 | convolution fusion | flops 10789060608 | bytes 74973184 | tf_op jit(solution)/shard_map/transpose(jvp())/dot_general | solution.py:10
  319.0 42.0 %fusion.3 = (bf16[4096,2048]{1,0:T(8,128)(2,1)}, bf16[4096,2048]{1,0:T(8,128)(2,1)}) fusion(f32[4096,2048]{1,0:T(8,128)} %fusion.43, f32[4096,2048]{1,0:T(8,128)} %get-tuple-element.21, bf16[4096,640]{0,1:T(8,128)(2,1)} %fusion.28, bf16[1,2048,640]{2,1,0:T(8,128)(2,1)S(1)} %copy-done.9), kind=kOutput, calls=%fused_computation.9 | convolution fusion | flops 10846470144 | bytes 108527616 | tf_op jit(solution)/shard_map/transpose(jvp())/dot_general | solution.py:10
  361.0 22.5 %fusion.54 = bf16[640,2048]{1,0:T(8,128)(2,1)} fusion(bf16[4096,2048]{1,0:T(8,128)(2,1)} %get-tuple-element.29, bf16[1,4096,640]{1,2,0:T(8,128)(2,1)} %copy.10, f32[4096]{0:T(1024)S(1)} %copy-done.3, f32[4096,2048]{1,0:T(8,128)} %fusion.43), kind=kOutput, calls=%fused_computation.65 | convolution fusion | flops 10796924928 | bytes 58212352 | tf_op jit(solution)/shard_map/transpose(jvp())/dot_general | solution.py:22
  383.5 22.4 %fusion.57 = bf16[640,2048]{1,0:T(8,128)(2,1)} fusion(bf16[4096,2048]{1,0:T(8,128)(2,1)} %convolution_convert_fusion.1, bf16[4096,640]{0,1:T(8,128)(2,1)} %get-tuple-element.23, f32[4096]{0:T(1024)S(1)} %copy-done.5, f32[4096,2048]{1,0:T(8,128)} %get-tuple-element.25), kind=kOutput, calls=%fused_computation.66 | convolution fusion | flops 10796924928 | bytes 58212352 | tf_op jit(solution)/shard_map/transpose(jvp())/dot_general | solution.py:22
  406.0 17.4 %fusion.48 = bf16[640,2048]{1,0:T(8,128)(2,1)} fusion(bf16[4096,2048]{1,0:T(8,128)(2,1)} %get-tuple-element.24, bf16[4096,640]{0,1:T(8,128)(2,1)} %get-tuple-element.23, f32[4096]{0:T(1024)S(1)} %copy-done.5), kind=kOutput, calls=%fused_computation.63 | convolution fusion | flops 10745282560 | bytes 24657920 | tf_op jit(solution)/shard_map/transpose(jvp())/dot_general | solution.py:21
  423.5 17.1 %fusion.45 = bf16[640,2048]{1,0:T(8,128)(2,1)} fusion(bf16[4096,2048]{1,0:T(8,128)(2,1)} %get-tuple-element.28, bf16[1,4096,640]{1,2,0:T(8,128)(2,1)} %copy.10, f32[4096]{0:T(1024)S(1)} %copy-done.3), kind=kOutput, calls=%fused_computation.62 | convolution fusion | flops 10745282560 | bytes 24657920 | tf_op jit(solution)/shard_map/transpose(jvp())/dot_general | solution.py:21
  440.7 17.3 %convolution_convert_fusion.3 = bf16[4096,640]{0,1:T(8,128)(2,1)} fusion(bf16[4096,2048]{1,0:T(8,128)(2,1)} %get-tuple-element.28, bf16[1,640,2048]{2,1,0:T(8,128)(2,1)} %all-gather.13.cloned.1.call-done), kind=kOutput, calls=%fused_computation.46 | convolution fusion | flops 10737418240 | bytes 24641536 | tf_op jit(solution)/shard_map/transpose(jvp())/dot_general | solution.py:21
  458.0 33.4 %reduce-scatter.9.cloned.1.call-done = bf16[160,2048]{1,0:T(8,128)(2,1)} async-done(((bf16[640,2048]{1,0:T(8,128)(2,1)}), bf16[160,2048]{1,0:T(8,128)(2,1)}) %reduce-scatter.9.cloned.1.call-update) | async-done | bytes 655376 | tf_op jit(solution)/shard_map/reduce_scatter | solution.py:31
  491.4 36.7 %reduce-scatter.7.cloned.1.call-done = bf16[160,2048]{1,0:T(8,128)(2,1)} async-done(((bf16[640,2048]{1,0:T(8,128)(2,1)}), bf16[160,2048]{1,0:T(8,128)(2,1)}) %reduce-scatter.7.cloned.1.call-update) | async-done | bytes 655376 | tf_op jit(solution)/shard_map/reduce_scatter | solution.py:31
  528.2 25.4 %fusion.17 = (f32[4096]{0:T(1024)S(1)}, bf16[4096,640]{0,1:T(8,128)(2,1)}) fusion(bf16[1,4096,640]{1,2,0:T(8,128)(2,1)} %copy.10, bf16[4096,640]{0,1:T(8,128)(2,1)} %convolution_convert_fusion.3, bf16[1,640,2048]{2,1,0:T(8,128)(2,1)S(1)} %copy-done.8, bf16[4096,2048]{1,0:T(8,128)(2,1)} %get-tuple-element.29, f32[4096,2048]{1,0:T(8,128)} %fusion.43), kind=kOutput, calls=%fused_computation.39 | convolution fusion | flops 10803474432 | bytes 68698112 | tf_op jit(solution)/shard_map/transpose(jvp())/dot_general | solution.py:22
  553.7 11.9 %fusion.27 = bf16[1,4096,640]{1,2,0:T(8,128)(2,1)} fusion(bf16[4096,640]{0,1:T(8,128)(2,1)} %fusion.28, bf16[4096,640]{0,1:T(8,128)(2,1)} %get-tuple-element.31, bf16[1,4096,640]{1,2,0:T(8,128)(2,1)} %copy.10, f32[4096]{0:T(1024)S(1)} %multiply_multiply_fusion, f32[4096]{0:T(1024)S(1)} %copy-done.3), kind=kLoop, calls=%fused_computation.52 | loop fusion | flops 18350080 | bytes 21004288 | tf_op jit(solution)/shard_map/broadcast_in_dim | solution.py:44
  565.6 7.8 %copy.11 = bf16[1,4096,640]{2,1,0:T(8,128)(2,1)} copy(bf16[1,4096,640]{1,2,0:T(8,128)(2,1)} %fusion.27) | data formatting | bytes 10485760
  573.4 107.8 %all-reduce.3.cloned.1.call-done = (bf16[1,160,2048]{2,1,0:T(8,128)(2,1)}, bf16[1,160,2048]{2,1,0:T(8,128)(2,1)}, bf16[1,160,2048]{2,1,0:T(8,128)(2,1)}, bf16[1,...) async-done(((bf16[1,160,2048]{2,1,0:T(8,128)(2,1)}, bf16[1,160,2048]{2,1,0:T(8,128)(2,1)}, bf16[1,160,2048]{2,1,0:T(8,128)(2,1)}, ...) | async-done | bytes 3932176 | tf_op jit(solution)/shard_map/psum | solution.py:31
  683.6 3.4 pad_maximum_fusion
  (61 shorter events, 10.6 us)
Async XLA Ops:
  7.2 30.9 %all-gather.13.cloned.1.call-start = ((), (), s32[]{:S(2)}) async-start(), calls=%async_computation.12 | async-start | bytes 3276800 | tf_op jit(solution)/shard_map/all_gather | solution.py:28
  9.7 55.2 %all-gather.15.cloned.1.call-start = ((), (), s32[]{:S(2)}) async-start(), calls=%async_computation.13 | async-start | bytes 3276800 | tf_op jit(solution)/shard_map/all_gather | solution.py:28
  12.3 86.3 %all-gather.17.cloned.1.call-start = ((), (), s32[]{:S(2)}) async-start(), calls=%async_computation.14 | async-start | bytes 3276800 | tf_op jit(solution)/shard_map/all_gather | solution.py:28
  14.9 103.5 %all-gather.21.cloned.1.call-start = ((), (), s32[]{:S(2)}) async-start(), calls=%async_computation.16 | async-start | bytes 3276800 | tf_op jit(solution)/shard_map/all_gather | solution.py:28
  15.4 130.1 %all-gather.23.cloned.1.call-start = ((), (), s32[]{:S(2)}) async-start(), calls=%async_computation.17 | async-start | bytes 3276800 | tf_op jit(solution)/shard_map/all_gather | solution.py:28
  16.0 156.8 %all-gather.19.cloned.1.call-start = ((), (), s32[]{:S(2)}) async-start(), calls=%async_computation.15 | async-start | bytes 3276800 | tf_op jit(solution)/shard_map/all_gather | solution.py:28
  16.6 441.4 %reduce-scatter.15.cloned.1.call-start = ((), (), s32[]{:S(2)}) async-start(), calls=%async_computation.10 | async-start | bytes 3276800 | tf_op jit(solution)/shard_map/reduce_scatter | solution.py:31
  28.1 0.6 copy-start
  28.7 36.2 %copy-start.2 = (f32[4096]{0:T(1024)}, f32[4096]{0:T(1024)S(1)}, u32[]{:S(2)}) copy-start(f32[4096]{0:T(1024)S(1)} %fusion.71) | copy-start | bytes 49156
  117.1 21.4 %copy-start.6 = (f32[4096]{0:T(1024)}, f32[4096]{0:T(1024)S(1)}, u32[]{:S(2)}) copy-start(f32[4096]{0:T(1024)S(1)} %get-tuple-element.22) | copy-start | bytes 49156
  117.1 142.8 %copy-start.4 = (f32[4096]{0:T(1024)}, f32[4096]{0:T(1024)S(1)}, u32[]{:S(2)}) copy-start(f32[4096]{0:T(1024)S(1)} %fusion.72) | copy-start | bytes 49156
  217.5 17.0 %copy-start.10 = (bf16[1,640,2048]{2,1,0:T(8,128)(2,1)S(1)}, bf16[1,640,2048]{2,1,0:T(8,128)(2,1)}, u32[]{:S(2)}) copy-start(bf16[1,640,2048]{2,1,0:T(8,128)(2,1)} %all-gather.23.cloned.1.call-done) | copy-start | bytes 7864324
  234.5 25.3 %copy-start.7 = (f32[4096]{0:T(1024)S(1)}, f32[4096]{0:T(1024)}, u32[]{:S(2)}) copy-start(f32[4096]{0:T(1024)} %copy-done.6) | copy-start | bytes 49156
  291.6 27.3 %copy-start.9 = (bf16[1,2048,640]{2,1,0:T(8,128)(2,1)S(1)}, bf16[1,2048,640]{2,1,0:T(8,128)(2,1)}, u32[]{:S(2)}) copy-start(bf16[1,2048,640]{2,1,0:T(8,128)(2,1)} %all-gather.17.cloned.1.call-done) | copy-start | bytes 7864324
  291.6 166.4 %reduce-scatter.17.cloned.1.call-start = ((), (), s32[]{:S(2)}) async-start(), calls=%async_computation.11 | async-start | bytes 3276800 | tf_op jit(solution)/shard_map/reduce_scatter | solution.py:31
  318.9 139.1 %reduce-scatter.11.cloned.1.call-start = ((), (), s32[]{:S(2)}) async-start(), calls=%async_computation.8 | async-start | bytes 3276800 | tf_op jit(solution)/shard_map/reduce_scatter | solution.py:31
  319.0 42.0 %copy-start.3 = (f32[4096]{0:T(1024)S(1)}, f32[4096]{0:T(1024)}, u32[]{:S(2)}) copy-start(f32[4096]{0:T(1024)} %copy-done.2) | copy-start | bytes 49156
  361.0 22.5 %copy-start.5 = (f32[4096]{0:T(1024)S(1)}, f32[4096]{0:T(1024)}, u32[]{:S(2)}) copy-start(f32[4096]{0:T(1024)} %copy-done.4) | copy-start | bytes 49156
  383.5 74.5 %reduce-scatter.13.cloned.1.call-start = ((), (), s32[]{:S(2)}) async-start(), calls=%async_computation.9 | async-start | bytes 3276800 | tf_op jit(solution)/shard_map/reduce_scatter | solution.py:31
  406.0 85.5 %reduce-scatter.9.cloned.1.call-start = ((), (), s32[]{:S(2)}) async-start(), calls=%async_computation.7 | async-start | bytes 3276800 | tf_op jit(solution)/shard_map/reduce_scatter | solution.py:31
  423.4 104.7 %reduce-scatter.7.cloned.1.call-start = ((), (), s32[]{:S(2)}) async-start(), calls=%async_computation.6 | async-start | bytes 3276800 | tf_op jit(solution)/shard_map/reduce_scatter | solution.py:31
  440.6 87.5 %copy-start.8 = (bf16[1,640,2048]{2,1,0:T(8,128)(2,1)S(1)}, bf16[1,640,2048]{2,1,0:T(8,128)(2,1)}, u32[]{:S(2)}) copy-start(bf16[1,640,2048]{2,1,0:T(8,128)(2,1)} %all-gather.15.cloned.1.call-done) | copy-start | bytes 7864324
  440.6 240.5 %all-reduce.3.cloned.1.call-start = ((), (), s32[]{:S(2)}) async-start(), calls=%async_computation.18 | async-start | bytes 7864320 | tf_op jit(solution)/shard_map/psum | solution.py:31
  528.2 25.5 %copy-start.1 = (f32[4096]{0:T(1024)S(1)}, f32[4096]{0:T(1024)}, u32[]{:S(2)}) copy-start(f32[4096]{0:T(1024)} %copy-done) | copy-start | bytes 49156
Sparse Core Ops, SparseCore 0:
  10.1 27.9 all-gather.12
  39.7 25.1 all-gather.14
  66.5 25.1 all-gather.16
  93.1 25.1 all-gather.20
  120.3 25.1 all-gather.22
  147.6 25.1 all-gather.18
  291.8 34.2 reduce-scatter.14
  328.6 34.2 reduce-scatter.16
  383.6 34.2 reduce-scatter.10
  420.3 34.2 reduce-scatter.12
  457.1 34.2 reduce-scatter.8
  493.8 34.2 reduce-scatter.6
  532.4 148.6 all-reduce.2
where the time goes:
time: 701 us; the launch traced here: 694 us
  matrix products  414 us (59%)
  waiting for transfers between devices  200 us (29%)
  other arithmetic  33.3 us (5%)
  local copies, waits for them, and re-layouts  31.8 us (5%)
  between operations  14.6 us (2%)
    dot_general x6, matrix products, layer(): up = jnp.dot(a, w['w_up'], preferred_element_type=jnp.float32)  151 us
    dot_general x6, matrix products, layer(): gate = jnp.dot(a, w['w_gate'], preferred_element_type=jnp.float32)  135 us
    dot_general x5, matrix products, matmul(): jnp.dot(a, w, preferred_element_type=jnp.float32).astype(jnp.bfloat16)  128 us
    psum x1, waiting for transfers between devices, summed(): lax.psum(lax.psum_scatter(term, 's', scatter_dimension=0, tiled=True), 'r')  108 us
    reduce_scatter x6, waiting for transfers between devices, summed(): lax.psum_scatter(term, 's', scatter_dimension=0, tiled=True)  70.1 us
    unnamed x25, local copies, waits for them, and re-layouts  24.3 us
    all_gather x6, waiting for transfers between devices, fetched(): lax.all_gather(w[number], 's', axis=0, tiled=True)  20.2 us
  transfers between devices with their start and end apart: 13, of which 8 were waited for; matrix products, arithmetic and copies ran while one was open for 51% of the time, Pallas kernels for 0%

commit v1 on v0

v1 whole, which is shorter than its diff:
```python
import jax
import jax.numpy as jnp
from jax import lax
from jax.experimental import pallas as pl
from jax.experimental.pallas import tpu as pltpu
from jax.sharding import PartitionSpec as P

T, D, F = 4096, 640, 2048
TB, FC = 512, 512
NB, J = T // TB, F // FC
STEPS = NB * J
XS, CS, YS, ZS = 2, 2, 2, 4
HR, QL = D // 8, FC // 4
SLOTS = 6
TICKS = 46
VMEM_LIMIT = 67_000_000
bf16, f32 = jnp.bfloat16, jnp.float32
NT = (((1,), (1,)), ((), ()))
MESH = pl.DeviceIdType.MESH


def dot(a, b):
    return jnp.dot(a, b, preferred_element_type=f32)


def dot_nt(a, b):
    return lax.dot_general(a, b, NT, preferred_element_type=f32)


def scale_of(wide):
    return lax.rsqrt(jnp.mean(wide * wide, -1, keepdims=True) + 1e-6)


def fwd_kernel(h_hbm, wg_hbm, wu_hbm, wd_hbm, o_hbm, h_v, a_v, yT_v, wg_v, wu_v, wd_v, wdT_v, s_v, sem, osem):
    copies = [
        pltpu.make_async_copy(src, dst, sem.at[i])
        for i, (src, dst) in enumerate([(h_hbm, h_v), (wg_hbm, wg_v), (wu_hbm, wu_v), (wd_hbm, wd_v)])
    ]
    for copy in copies:
        copy.start()
    yT_v[...] = jnp.zeros_like(yT_v)
    s_v[1] = jnp.zeros_like(s_v[1])
    copies[0].wait()

    @pl.loop(0, NB)
    def _(t):
        wide = h_v[t].astype(f32)
        a_v[t] = (wide * scale_of(wide)).astype(bf16)

    for copy in copies[1:]:
        copy.wait()

    @pl.loop(0, J)
    def _(j):
        wdT_v[j] = wd_v[j].T

    def front(j, t):
        return dot(a_v[t], wg_v[j]), dot(a_v[t], wu_v[j])

    def mid(gate, up):
        return (gate * jax.nn.sigmoid(gate) * up).astype(bf16)

    def back(j, t, act):
        yT_v[t] += dot_nt(wdT_v[j], act)

    @pl.loop(0, STEPS // 2)
    def _(pair):
        i = 2 * pair
        before = jnp.maximum(i - 1, 0)
        first = front(i // NB, i % NB)
        back(before // NB, before % NB, s_v[1])
        s_v[0] = mid(*first)
        second = front((i + 1) // NB, (i + 1) % NB)
        back(i // NB, i % NB, s_v[0])
        s_v[1] = mid(*second)

    back(J - 1, NB - 1, s_v[1])

    @pl.loop(0, NB)
    def _(t):
        h_v[t] = h_v[t] + yT_v[t].astype(bf16).T

    copy = pltpu.make_async_copy(h_v, o_hbm, osem)
    copy.start()
    copy.wait()


def forward(h, wg, wu, wd):
    anywhere = pl.BlockSpec(memory_space=pl.ANY)
    return pl.pallas_call(
        fwd_kernel,
        out_shape=jax.ShapeDtypeStruct((NB, TB, D), bf16),
        in_specs=[anywhere] * 4,
        out_specs=anywhere,
        scratch_shapes=[
            pltpu.VMEM((NB, TB, D), bf16),
            pltpu.VMEM((NB, TB, D), bf16),
            pltpu.VMEM((NB, D, TB), f32),
            pltpu.VMEM((J, D, FC), bf16),
            pltpu.VMEM((J, D, FC), bf16),
            pltpu.VMEM((J, FC, D), bf16),
            pltpu.VMEM((J, D, FC), bf16),
            pltpu.VMEM((2, TB, FC), bf16),
            pltpu.SemaphoreType.DMA((4,)),
            pltpu.SemaphoreType.DMA,
        ],
        compiler_params=pltpu.CompilerParams(vmem_limit_bytes=VMEM_LIMIT),
        cost_estimate=pl.CostEstimate(flops=6 * T * D * F, bytes_accessed=20_000_000, transcendentals=0),
        name="forward",
    )(h, wg, wu, wd)


class Reduction:
    def __init__(self, g1_hbm, g0_hbm, out_hbm, gbuf, drecv, xs, xrecv, ys, yrecv, keep, zs, zrecv, fq, dsem, xsem, ysem, zsem, fsem, asem, lsem, psem, near):
        self.__dict__.update({k: v for k, v in locals().items() if k != "self"})
        r, s = lax.axis_index("r"), lax.axis_index("s")
        self.y, self.z, self.x, self.c = r // ZS, r % ZS, s // CS, s % CS
        self.partner = {"s": self.x * CS + 1 - self.c}
        self.xpeer = {"s": (1 - self.x) * CS + self.c}
        self.ypeer = {"r": (1 - self.y) * ZS + self.z}
        self.zpeers = [{"r": self.y * ZS + (self.z + d) % ZS} for d in range(1, ZS)]
        self.peers = [self.partner, self.xpeer, self.ypeer, *self.zpeers]

    def enter(self):
        barrier = pltpu.get_barrier_semaphore()
        for peer in self.peers:
            pl.semaphore_signal(barrier, inc=1, device_id=peer, device_id_type=MESH)
        pl.semaphore_wait(barrier, len(self.peers))

    def load(self, g):
        return pltpu.make_async_copy(self.g1_hbm.at[g], self.gbuf.at[g % 2], self.psem)

    def load0(self, g):
        return pltpu.make_async_copy(self.g0_hbm.at[g - J], self.gbuf.at[g % 2], self.psem)

    def at(self, k):
        block = k // 4
        return (k >= 0) & (k % 4 < 3) & (block != 6) & (block < 9), block - jnp.where(block > 6, 1, 0), k % 4

    def remote(self, src, dst, sems, peer):
        return pltpu.make_async_remote_copy(src, dst, sems.at[0], sems.at[1], device_id=peer, device_id_type=MESH)

    def dcopy(self, b, m, slot):
        return self.remote(self.gbuf.at[b, m, 1 - self.c], self.drecv.at[slot], self.dsem.at[slot], self.partner)

    def xcopy(self, slot):
        return self.remote(self.xs.at[slot], self.xrecv.at[slot], self.xsem.at[slot], self.xpeer)

    def ycopy(self, slot):
        return self.remote(self.ys.at[slot], self.yrecv.at[slot], self.ysem.at[slot], self.ypeer)

    def zcopies(self, slot):
        return [self.remote(self.zs.at[slot, i], self.zrecv.at[slot, i], self.zsem.at[slot, i], peer) for i, peer in enumerate(self.zpeers)]

    def fcopies(self, g, m, slot):
        place = self.out_hbm.at[g, m, self.y, self.z]
        return [self.remote(self.fq.at[slot], place, self.fsem.at[slot, i], peer) for i, peer in enumerate(self.zpeers)] + [
            pltpu.make_async_copy(self.fq.at[slot], place, self.lsem.at[slot])
        ]

    def acopy(self, g, m, slot):
        half = self.out_hbm.at[g, m, self.y]
        return self.remote(half, half, self.asem.at[slot], self.ypeer)

    def stage(self, k, delay, body):
        valid, g, m = self.at(k - delay)

        @pl.when(valid)
        def _():
            body(g, m, (k - delay) % SLOTS)

    def tick(self, k):
        x, c, y, z = self.x, self.c, self.y, self.z
        gbuf, drecv, xrecv, keep = self.gbuf, self.drecv, self.xrecv, self.keep

        @pl.when(k >= 2)
        def _():
            for i in range(len(self.peers)):
                pl.semaphore_wait(self.near.at[i], 1)

        ahead = k + 2
        block = ahead // 4
        turn = (ahead % 4 == 0) & (k >= 0)

        @pl.when(turn & (block < J))
        def _():
            self.load(block).start()

        @pl.when(turn & (block >= J) & (block < 8) & (block != 6))
        def _():
            self.load0(block - jnp.where(block > 6, 1, 0)).start()

        def end(g, m, slot):
            self.acopy(g, m, slot).wait()

        def gather_y(g, m, slot):
            for copy in self.fcopies(g, m, slot):
                copy.wait()
            self.acopy(g, m, slot).start()

        def finish(g, m, slot):
            for copy in self.zcopies(slot):
                copy.wait()
            total = keep[slot, z]
            for i in range(ZS - 1):
                total += self.zrecv[slot, i].astype(f32)
            self.fq[slot] = total.astype(bf16)
            for copy in self.fcopies(g, m, slot):
                copy.start()

        def to_z(g, m, slot):
            self.ycopy(slot).wait()
            keep[slot] += self.yrecv[slot].astype(f32)
            for i in range(ZS - 1):
                self.zs[slot, i] = keep[slot, (z + i + 1) % ZS].astype(bf16)
            for copy in self.zcopies(slot):
                copy.start()

        def to_y(g, m, slot):
            self.xcopy(slot).wait()

            def total(half):
                return gbuf[g % 2, m, c, x, half].astype(f32) + drecv[slot, x, half].astype(f32) + xrecv[slot, half].astype(f32)

            self.ys[slot] = total(1 - y).astype(bf16)
            self.ycopy(slot).start()
            keep[slot] = total(y)

        def to_x(g, m, slot):
            self.dcopy(g % 2, m, slot).wait()
            self.xs[slot] = (gbuf[g % 2, m, c, 1 - x].astype(f32) + drecv[slot, 1 - x].astype(f32)).astype(bf16)
            self.xcopy(slot).start()

        def to_partner(g, m, slot):
            @pl.when((m == 0) & (g < J))
            def _():
                self.load(g).wait()

            @pl.when((m == 0) & (g >= J) & (g < 2 * J - 1))
            def _():
                self.load0(g).wait()

            self.dcopy(g % 2, m, slot).start()

        self.stage(k, 11, end)
        self.stage(k, 9, gather_y)
        self.stage(k, 7, finish)
        self.stage(k, 5, to_z)
        self.stage(k, 3, to_y)
        self.stage(k, 1, to_x)
        self.stage(k, 0, to_partner)

        @pl.when(k < TICKS - 2)
        def _():
            for i, peer in enumerate(self.peers):
                pl.semaphore_signal(self.near.at[i], inc=1, device_id=peer, device_id_type=MESH)


def bwd_kernel(reduce, *refs):
    h_hbm, dy_hbm, wg_hbm, wu_hbm, wd_hbm, *refs = refs
    g1_hbm, dh_hbm, g_hbm, *refs = refs if reduce else (None, *refs)
    out_hbm, *refs = refs if reduce else (None, *refs)
    dy_v, a_v, aT_v, dyT_v, daT_v, wg_v, wu_v, wd_v, acc_v, gb_v, s_v, sem, gsem, hsem, *refs = refs
    copies = [
        pltpu.make_async_copy(src, dst, sem.at[i])
        for i, (src, dst) in enumerate([(h_hbm, a_v), (dy_hbm, dy_v), (wg_hbm, wg_v), (wu_hbm, wu_v), (wd_hbm, wd_v)])
    ]
    for copy in copies:
        copy.start()
    red = None
    if reduce:
        red = Reduction(g1_hbm, g_hbm, out_hbm, *refs)
        red.load(0).start()
        red.enter()
    acc_v[...] = jnp.zeros_like(acc_v)
    daT_v[...] = jnp.zeros_like(daT_v)
    s_v[1] = jnp.zeros_like(s_v[1])
    copies[0].wait()
    copies[1].wait()

    @pl.loop(0, NB)
    def _(t):
        wide = a_v[t].astype(f32)
        a = (wide * scale_of(wide)).astype(bf16)
        a_v[t] = a
        aT_v[t] = a.T
        dyT_v[t] = dy_v[t].T

    for copy in copies[2:]:
        copy.wait()

    def front(j, t):
        return dot(a_v[t], wg_v[j]), dot(a_v[t], wu_v[j]), dot_nt(dy_v[t], wd_v[j])

    def mid(slot, gate, up, dact):
        dact = dact.astype(bf16).astype(f32)
        sg = jax.nn.sigmoid(gate)
        s = gate * sg
        s_v[slot, 0] = (s * up).astype(bf16)
        s_v[slot, 1] = (dact * up * (sg + s * (1.0 - sg))).astype(bf16)
        s_v[slot, 2] = (dact * s).astype(bf16)

    def back(j, t, slot):
        act, dgate, dup = s_v[slot, 0], s_v[slot, 1], s_v[slot, 2]
        daT_v[t] += dot_nt(wg_v[j], dgate) + dot_nt(wu_v[j], dup)
        acc_v[0] += dot(aT_v[t], dgate)
        acc_v[1] += dot(aT_v[t], dup)
        acc_v[2] += dot(dyT_v[t], act)

    def flush(dst):
        for x in range(XS):
            for c in range(CS):
                n = x * CS + c
                for h in range(2):
                    for q in range(4):
                        rows = slice(n * 2 * HR + h * HR, n * 2 * HR + (h + 1) * HR)
                        for m in range(2):
                            dst[m, c, x, h, q] = acc_v[m, rows, q * QL : (q + 1) * QL].astype(bf16)
                        rows = slice(q * 2 * HR + h * HR, q * 2 * HR + (h + 1) * HR)
                        dst[2, c, x, h, q] = acc_v[2, rows, n * QL : (n + 1) * QL].astype(bf16)

    def put(j):
        return pltpu.make_async_copy(gb_v, g_hbm.at[j], gsem)

    @pl.loop(0, STEPS // 2)
    def _(pair):
        i = 2 * pair
        before = jnp.maximum(i - 1, 0)
        first = front(i // NB, i % NB)
        back(before // NB, before % NB, 1)
        mid(0, *first)

        @pl.when((i % NB == 0) & (pair > 0))
        def _():
            flush(gb_v)
            put(before // NB).start()
            acc_v[...] = jnp.zeros_like(acc_v)

        if reduce:
            red.tick(i)
        second = front((i + 1) // NB, (i + 1) % NB)
        back(i // NB, i % NB, 0)
        mid(1, *second)

        @pl.when((i % NB == 0) & (pair > 0))
        def _():
            put(before // NB).wait()

        if reduce:
            red.tick(i + 1)

    reload = pltpu.make_async_copy(h_hbm, a_v, hsem)
    reload.start()
    back(J - 1, NB - 1, 1)
    if reduce:
        flush(red.gbuf.at[1])
    else:
        flush(gb_v)
        put(J - 1).start()
    reload.wait()

    @pl.loop(0, NB)
    def _(t):
        if reduce:
            red.tick(STEPS + t)
        da = daT_v[t].astype(bf16).T.astype(f32)
        wide = a_v[t].astype(f32)
        scale = scale_of(wide)
        mean = jnp.mean(da * wide, -1, keepdims=True)
        dy_v[t] = dy_v[t] + (da * scale - wide * (scale * scale * scale * mean)).astype(bf16)

    copy = pltpu.make_async_copy(dy_v, dh_hbm, hsem)
    copy.start()
    if reduce:

        @pl.loop(STEPS + NB, TICKS)
        def _(k):
            red.tick(k)

    else:
        put(J - 1).wait()
    copy.wait()


def backward(h, dy, wg, wu, wd, g1=None):
    reduce = g1 is not None
    anywhere = pl.BlockSpec(memory_space=pl.ANY)
    tokens, turned, grads = (NB, TB, D), (NB, D, TB), (J, 3, CS, XS, 2, 4, HR, QL)
    outs = [jax.ShapeDtypeStruct(tokens, bf16), jax.ShapeDtypeStruct(grads, bf16)]
    scratch = [
        pltpu.VMEM(tokens, bf16),
        pltpu.VMEM(tokens, bf16),
        pltpu.VMEM(turned, bf16),
        pltpu.VMEM(turned, bf16),
        pltpu.VMEM(turned, f32),
        pltpu.VMEM((J, D, FC), bf16),
        pltpu.VMEM((J, D, FC), bf16),
        pltpu.VMEM((J, FC, D), bf16),
        pltpu.VMEM((3, D, FC), f32),
        pltpu.VMEM(grads[1:], bf16),
        pltpu.VMEM((2, 3, TB, FC), bf16),
        pltpu.SemaphoreType.DMA((5,)),
        pltpu.SemaphoreType.DMA,
        pltpu.SemaphoreType.DMA,
    ]
    if reduce:
        piece = (2, 4, HR, QL)
        outs.append(jax.ShapeDtypeStruct((2 * J, 3, *piece), bf16))
        pair = pltpu.SemaphoreType.DMA((SLOTS, 2))
        triple = pltpu.SemaphoreType.DMA((SLOTS, ZS - 1, 2))
        scratch += [
            pltpu.VMEM((2, *grads[1:]), bf16),
            pltpu.VMEM((SLOTS, XS, *piece), bf16),
            pltpu.VMEM((SLOTS, *piece), bf16),
            pltpu.VMEM((SLOTS, *piece), bf16),
            pltpu.VMEM((SLOTS, *piece[1:]), bf16),
            pltpu.VMEM((SLOTS, *piece[1:]), bf16),
            pltpu.VMEM((SLOTS, *piece[1:]), f32),
            pltpu.VMEM((SLOTS, ZS - 1, *piece[2:]), bf16),
            pltpu.VMEM((SLOTS, ZS - 1, *piece[2:]), bf16),
            pltpu.VMEM((SLOTS, *piece[2:]), bf16),
            pair,
            pair,
            pair,
            triple,
            triple,
            pair,
            pltpu.SemaphoreType.DMA((SLOTS,)),
            pltpu.SemaphoreType.DMA,
            pltpu.SemaphoreType.REGULAR((6,)),
        ]
    args = (h, dy, wg, wu, wd) + ((g1,) if reduce else ())
    return pl.pallas_call(
        lambda *refs: bwd_kernel(reduce, *refs),
        out_shape=tuple(outs),
        in_specs=[anywhere] * len(args),
        out_specs=(anywhere,) * len(outs),
        scratch_shapes=scratch,
        compiler_params=pltpu.CompilerParams(
            vmem_limit_bytes=VMEM_LIMIT, **(dict(collective_id=1, has_side_effects=True) if reduce else {})
        ),
        cost_estimate=pl.CostEstimate(flops=16 * T * D * F, bytes_accessed=30_000_000, transcendentals=0),
        name="backward_reduce" if reduce else "backward",
    )(*args)


def solution(mesh):
    def step(x, dy, *weights):
        def fetched(l):
            wg, wu, wd = [lax.all_gather(w[l], "s", axis=0, tiled=True) for w in weights]
            cols = [w.reshape(D, 4, J, QL).transpose(2, 0, 1, 3).reshape(J, D, FC) for w in (wg, wu)]
            return (*cols, wd.reshape(4, J, QL, D).transpose(1, 0, 2, 3).reshape(J, FC, D))

        w0, w1 = fetched(0), fetched(1)
        h0, dy = x.reshape(NB, TB, D), dy.reshape(NB, TB, D)
        h1 = forward(h0, *w0)
        dh1, g1 = backward(h1, dy, *w1)
        dx, _, total = backward(h0, dh1, *w0, g1)
        total = total.reshape(2, J, 3, 2, 4, HR, QL)[::-1]
        cols = [total[:, :, m].transpose(0, 2, 4, 3, 1, 5).reshape(2, 2 * HR, F) for m in range(2)]
        down = total[:, :, 2].transpose(0, 1, 5, 3, 2, 4).reshape(2, F // 4, D)
        return dx.reshape(1, T, D), *cols, down

    states, cut = P(("rep", "r", "s"), None, None), P(None, "s", None)
    return jax.shard_map(
        step,
        mesh=mesh,
        in_specs=(states, states) + (cut,) * 3,
        out_specs=(states,) + (P("rep", "s", None),) * 3,
        check_vma=False,
    )
```

time: 701 us -> 553 us (0.79)
  matrix products: 414 us -> 0 us
  Pallas kernels: 0 us -> 338 us
  waiting for transfers between devices: 200 us -> 109 us
  local copies, waits for them, and re-layouts: 31.8 us -> 80.8 us
  other arithmetic: 33.3 us -> 0 us
    dot_general x17 -> x0, matrix products: 414 us -> none  [the longest x6 151 us: layer(): up = jnp.dot(a, w['w_up'], preferred_element_type=jnp.float32)]
    pallas_call x0 -> x3, Pallas kernels: none -> 338 us  [the longest x2 288 us: backward(): pl.pallas_call(lambda *refs: bwd_kernel(reduce, *refs), out_shape=tuple(o...]
    psum x1 -> x0, waiting for transfers between devices: 108 us -> none  [summed(): lax.psum(lax.psum_scatter(term, 's', scatter_dimension=0, tiled=True), 'r')]
    all_gather x6, waiting for transfers between devices: 20.2 us -> 107 us  [fetched(): lax.all_gather(w[l], 's', axis=0, tiled=True)]
    reduce_scatter x6 -> x0, waiting for transfers between devices: 70.1 us -> none  [summed(): lax.psum_scatter(term, 's', scatter_dimension=0, tiled=True)]
    reshape x0 -> x17, local copies, waits for them, and re-layouts: none -> 58.8 us  [the longest x12 47.5 us: fetched(): w.reshape(D, 4, J, QL).transpose(2, 0, 1, 3).reshape(J, D, FC)]
    unnamed x25 -> x7, local copies, waits for them, and re-layouts: 24.3 us -> 7.99 us
    broadcast_in_dim x1 -> x0, other arithmetic: 11.9 us -> none  [step(): by_h[None]]
  transfers between devices with their start and end apart: 13 -> 6, of which waited for: 8 -> 6; matrix products, arithmetic and copies ran while one was open for 51% -> 10% of each run, Pallas kernels for 0% -> 0%
where the time goes in v1:
time: 553 us; the launch traced here: 543 us
  Pallas kernels  338 us (61%)
  waiting for transfers between devices  109 us (20%)
  local copies, waits for them, and re-layouts  80.8 us (15%)
  between operations  14.7 us (3%)
    pallas_call x2, Pallas kernels, backward(): pl.pallas_call(lambda *refs: bwd_kernel(reduce, *refs), out_shape=tuple(o...  288 us
    all_gather x6, waiting for transfers between devices, fetched(): lax.all_gather(w[l], 's', axis=0, tiled=True)  107 us
    pallas_call x1, Pallas kernels, forward(): pl.pallas_call(fwd_kernel, out_shape=jax.ShapeDtypeStruct((NB, TB, D), bf...  50.1 us
    reshape x12, local copies, waits for them, and re-layouts, fetched(): w.reshape(D, 4, J, QL).transpose(2, 0, 1, 3).reshape(J, D, FC)  47.5 us
  transfers between devices with their start and end apart: 6, of which 6 were waited for; matrix products, arithmetic and copies ran while one was open for 10% of the time, Pallas kernels for 0%

profile of v1, /device:TPU:0, one launch (start us, length us, event | category | flops | bytes accessed | tf_op | source)
XLA Modules:
  0.0 543.3 jit_solution(15335249460004481762)
XLA Ops:
  7.2 2.6 fusion.3
  10.6 1.2 fusion.2
  12.4 1.2 fusion.1
  14.2 23.9 %all-gather.19.cloned.1.call-done = bf16[1,640,2048]{2,1,0:T(8,128)(2,1)} async-done(((bf16[1,160,2048]{2,1,0:T(8,128)(2,1)}), bf16[1,640,2048]{2,1,0:T(8,128)(2,1)}) %all-gather.19.cloned.1.call-update) | async-done | bytes 2621456 | tf_op jit(solution)/shard_map/all_gather | solution.py:450
  38.1 4.2 reshape.73
  42.3 2.5 copy.34
  44.9 5.1 reshape.74.refs_2_
  50.0 15.5 %all-gather.13.cloned.1.call-done = bf16[1,640,2048]{2,1,0:T(8,128)(2,1)} async-done(((bf16[1,160,2048]{2,1,0:T(8,128)(2,1)}), bf16[1,640,2048]{2,1,0:T(8,128)(2,1)}) %all-gather.13.cloned.1.call-update) | async-done | bytes 2621456 | tf_op jit(solution)/shard_map/all_gather | solution.py:450
  65.5 4.2 reshape.66
  69.7 2.5 copy.36
  72.2 5.1 reshape.67.wg_hbm.refs_2_
  77.4 15.5 %all-gather.21.cloned.1.call-done = bf16[1,640,2048]{2,1,0:T(8,128)(2,1)} async-done(((bf16[1,160,2048]{2,1,0:T(8,128)(2,1)}), bf16[1,640,2048]{2,1,0:T(8,128)(2,1)}) %all-gather.21.cloned.1.call-update) | async-done | bytes 2621456 | tf_op jit(solution)/shard_map/all_gather | solution.py:450
  92.9 4.2 reshape.75
  97.1 2.5 copy.33
  99.6 5.2 reshape.76.refs_3_
  104.8 14.8 %all-gather.15.cloned.1.call-done = bf16[1,640,2048]{2,1,0:T(8,128)(2,1)} async-done(((bf16[1,160,2048]{2,1,0:T(8,128)(2,1)}), bf16[1,640,2048]{2,1,0:T(8,128)(2,1)}) %all-gather.15.cloned.1.call-update) | async-done | bytes 2621456 | tf_op jit(solution)/shard_map/all_gather | solution.py:450
  119.5 4.2 reshape.68
  123.8 2.5 copy.35
  126.3 5.1 reshape.69.wu_hbm.refs_3_
  131.4 14.8 %all-gather.23.cloned.1.call-done = bf16[1,2048,640]{2,1,0:T(8,128)(2,1)} async-done(((bf16[1,512,640]{2,1,0:T(8,128)(2,1)}), bf16[1,2048,640]{2,1,0:T(8,128)(2,1)}) %all-gather.23.cloned.1.call-update) | async-done | bytes 2621456 | tf_op jit(solution)/shard_map/all_gather | solution.py:450
  146.2 3.6 copy.23
  149.7 23.1 %all-gather.17.cloned.1.call-done = bf16[1,2048,640]{2,1,0:T(8,128)(2,1)} async-done(((bf16[1,512,640]{2,1,0:T(8,128)(2,1)}), bf16[1,2048,640]{2,1,0:T(8,128)(2,1)}) %all-gather.17.cloned.1.call-update) | async-done | bytes 2621456 | tf_op jit(solution)/shard_map/all_gather | solution.py:450
  172.8 3.6 copy.20
  176.4 50.1 %forward.1.refs_0_ = bf16[8,512,640]{2,1,0:T(8,128)(2,1)} custom-call(bf16[8,512,640]{2,1,0:T(8,128)(2,1)} %bitcast.50, bf16[4,640,512]{2,1,0:T(8,128)(2,1)} %reshape.67.wg_hbm.refs_2_, bf16[4,640,512]{2,1,0:T(8,128)(2,1)} %reshape.69.wu_hbm.refs_3_, bf16[4,512,640]{2,1,0:T(8,128)(2,1)} %bitcast.46), custom_call_target="tpu_custom_call" | custom-call | flops 32212254720 | bytes 20000000 | tf_op jit(solution)/shard_map/forward/pallas_call | solution.py:90
  226.5 124.3 %backward.1 = (bf16[8,512,640]{2,1,0:T(8,128)(2,1)}, bf16[4,3,2,2,2,4,80,128]{7,6,5,4,3,2,1,0:T(8,128)(2,1)}) custom-call(bf16[8,512,640]{2,1,0:T(8,128)(2,1)} %forward.1.refs_0_, bf16[8,512,640]{2,1,0:T(8,128)(2,1)} %bitcast.49, bf16[4,640,512]{2,1,0:T(8,128)(2,1)} %reshape.74.refs_2_, bf16[4,640,512]{2,1,0:T(8,128)(2,1)} %reshape.76.refs_3_, ...), custom_call_target="tpu_custom_call" | custom-call | flops 85899345920 | bytes 30000000 | tf_op jit(solution)/shard_map/backward/pallas_call | solution.py:433
  350.9 163.9 %backward_reduce.1 = (bf16[8,512,640]{2,1,0:T(8,128)(2,1)}, bf16[4,3,2,2,2,4,80,128]{7,6,5,4,3,2,1,0:T(8,128)(2,1)}, bf16[8,3,2,4,80,128]{5,4,3,2,1,0:T(8,128)(2,1)}) custom-call(bf16[8,512,640]{2,1,0:T(8,128)(2,1)} %bitcast.51, bf16[8,512,640]{2,1,0:T(8,128)(2,1)} %get-tuple-element.8.refs_1_, bf16[4,640,512]{2,1,0:T(8,128)(2,1)} %reshape.67.wg_hbm.refs_2_, ...), custom_call_target="tpu_custom_call" | custom-call | flops 85899345920 | bytes 30000000 | tf_op jit(solution)/shard_map/backward_reduce/pallas_call | solution.py:433
  514.8 4.5 fusion
  521.4 1.7 copy.27
  523.1 1.9 reverse_bitcast_fusion.1
  526.0 1.8 reshape.82
  528.9 1.8 reshape.81
  530.7 5.3 copy.38
  (21 shorter events, 6.1 us)
Async XLA Ops:
  7.2 3.5 copy-start
  7.2 30.9 %all-gather.19.cloned.1.call-start = ((), (), s32[]{:S(2)}) async-start(), calls=%async_computation.3 | async-start | bytes 3276800 | tf_op jit(solution)/shard_map/all_gather | solution.py:450
  9.8 2.6 copy-start.1
  9.8 55.7 %all-gather.13.cloned.1.call-start = ((), (), s32[]{:S(2)}) async-start(), calls=%async_computation | async-start | bytes 3276800 | tf_op jit(solution)/shard_map/all_gather | solution.py:450
  10.6 82.3 %all-gather.21.cloned.1.call-start = ((), (), s32[]{:S(2)}) async-start(), calls=%async_computation.4 | async-start | bytes 3276800 | tf_op jit(solution)/shard_map/all_gather | solution.py:450
  11.8 107.7 %all-gather.15.cloned.1.call-start = ((), (), s32[]{:S(2)}) async-start(), calls=%async_computation.1 | async-start | bytes 3276800 | tf_op jit(solution)/shard_map/all_gather | solution.py:450
  12.4 133.8 %all-gather.23.cloned.1.call-start = ((), (), s32[]{:S(2)}) async-start(), calls=%async_computation.5 | async-start | bytes 3276800 | tf_op jit(solution)/shard_map/all_gather | solution.py:450
  13.7 159.2 %all-gather.17.cloned.1.call-start = ((), (), s32[]{:S(2)}) async-start(), calls=%async_computation.2 | async-start | bytes 3276800 | tf_op jit(solution)/shard_map/all_gather | solution.py:450
Sparse Core Ops, SparseCore 0:
  10.1 27.9 all-gather.18
  40.2 25.1 all-gather.12
  67.6 25.1 all-gather.20
  94.3 25.1 all-gather.14
  120.9 25.1 all-gather.22
  147.6 25.1 all-gather.16

commit v2 on v1

--- a/solution.py
+++ b/solution.py
@@ -10,7 +10,8 @@
 NB, J = T // TB, F // FC
 STEPS = NB * J
 XS, CS, YS, ZS = 2, 2, 2, 4
-HR, QL = D // 8, FC // 4
+HR, DR, QL = D // 8, FC // 8, FC // 4
+GATE_UP, DOWN = (2, J, 4, 2, HR, FC), (J, 4, 2, DR, D)
 SLOTS = 6
 TICKS = 46
 VMEM_LIMIT = 67_000_000
@@ -31,31 +32,171 @@
     return lax.rsqrt(jnp.mean(wide * wide, -1, keepdims=True) + 1e-6)
 
 
-def fwd_kernel(h_hbm, wg_hbm, wu_hbm, wd_hbm, o_hbm, h_v, a_v, yT_v, wg_v, wu_v, wd_v, wdT_v, s_v, sem, osem):
-    copies = [
-        pltpu.make_async_copy(src, dst, sem.at[i])
-        for i, (src, dst) in enumerate([(h_hbm, h_v), (wg_hbm, wg_v), (wu_hbm, wu_v), (wd_hbm, wd_v)])
-    ]
+class Gather:
+    def __init__(self, args, outs, w_v, own, lsem, osem, isem, psem, xsem, rsem, esem):
+        self.__dict__.update({k: v for k, v in locals().items() if k != "self"})
+        r, s = lax.axis_index("r"), lax.axis_index("s")
+        self.r, self.s, self.y, self.z, x, c = r, s, r // ZS, r % ZS, s // CS, s % CS
+        self.far = (1 - x) * CS + c
+        self.partner = {"s": x * CS + 1 - c}
+        self.xpeer = {"s": self.far}
+        self.ypeer = {"r": (1 - self.y) * ZS + self.z}
+        self.zpeers = [{"r": self.y * ZS + (self.z + d) % ZS} for d in range(1, ZS)]
+
+    def enter(self):
+        barrier = pltpu.get_barrier_semaphore()
+        peers = [self.partner, self.xpeer, self.ypeer, *self.zpeers]
+        for peer in peers:
+            pl.semaphore_signal(barrier, inc=1, device_id=peer, device_id_type=MESH)
+        pl.semaphore_wait(barrier, len(peers))
+
+    def remote(self, src, dst, sems, peer):
+        return pltpu.make_async_remote_copy(src, dst, sems.at[0], sems.at[1], device_id=peer, device_id_type=MESH)
+
+    def mine(self, layer):
+        wg, wu, wd = self.args
+        copies, n = [], 0
+        for j in range(J):
+            gu, down = (self.w_v[0].at[:, j, self.s], self.w_v[1].at[j, self.s]) if layer == 0 else (self.own[0].at[:, j], self.own[1].at[j])
+            for m, w in enumerate((wg, wu)):
+                for q in range(4):
+                    for h in range(2):
+                        part = w.at[layer, pl.ds(h * HR, HR), pl.ds(q * FC + j * QL, QL)]
+                        copies.append(pltpu.make_async_copy(part, gu.at[m, h, :, pl.ds(q * QL, QL)], self.lsem.at[layer, n]))
+                        n += 1
+            for h in range(2):
+                part = wd.at[layer, pl.ds(j * QL + h * DR, DR), :]
+                copies.append(pltpu.make_async_copy(part, down.at[h], self.lsem.at[layer, n]))
+                n += 1
+        return copies
+
+    def hand(self, kind, j):
+        s = self.far if kind == 2 else self.s
+        peer = self.xpeer if kind == 1 else self.partner
+        return [
+            self.remote(ref, ref, self.psem.at[kind, j, n], peer)
+            for n, ref in enumerate((self.w_v[0].at[:, j, s], self.w_v[1].at[j, s]))
+        ]
+
+    def save0(self, j):
+        return [pltpu.make_async_copy(self.w_v[0].at[:, j], self.outs[0].at[:, j], self.osem.at[j, 0]), pltpu.make_async_copy(self.w_v[1].at[j], self.outs[1].at[j], self.osem.at[j, 1])]
+
+    def own1(self):
+        gu, down = self.outs[2].at[:, :, self.s], self.outs[3].at[:, self.s]
+        return [
+            pltpu.make_async_copy(self.own[0], gu, self.isem.at[0]),
+            pltpu.make_async_copy(self.own[1], down, self.isem.at[1]),
+            self.remote(self.own[0], gu, self.esem.at[0], self.partner),
+            self.remote(self.own[1], down, self.esem.at[1], self.partner),
+        ]
+
+    def x1(self):
+        j, h = self.r // 2, self.r % 2
+        return [
+            self.remote(self.own[0].at[:, j, h], self.outs[2].at[:, j, self.s, h], self.xsem.at[0], self.xpeer),
+            self.remote(self.own[1].at[j, h], self.outs[3].at[j, self.s, h], self.xsem.at[1], self.xpeer),
+        ]
+
+    def z1(self):
+        j, h = self.r // 2, self.r % 2
+        refs = (self.outs[2].at[:, j, self.far, h], self.outs[3].at[j, self.far, h])
+        return [self.remote(ref, ref, self.rsem.at[i, n], peer) for i, peer in enumerate(self.zpeers) for n, ref in enumerate(refs)]
+
+    def part(self, y, sems, peer):
+        refs = (self.outs[2].at[:, pl.ds(2 * y, 2), self.far], self.outs[3].at[pl.ds(2 * y, 2), self.far])
+        return [self.remote(ref, ref, self.esem.at[sems + n], peer) for n, ref in enumerate(refs)]
+
+    def y1(self):
+        return self.part(self.y, 2, self.ypeer)
+
+    def p1(self):
+        return self.part(self.y, 4, self.partner)
+
+    def p2(self):
+        return self.part(1 - self.y, 6, self.partner)
+
+    def tick(self, i):
+        @pl.when(i == 2)
+        def _():
+            wait(self.x1())
+            start(self.z1())
+
+        @pl.when(i == 18)
+        def _():
+            wait(self.z1())
+            start(self.y1())
+            start(self.p1())
+
+        for j in range(1, J):
+
+            @pl.when(i == NB * j - 2)
+            def _():
+                wait(self.hand(1, j))
+                start(self.hand(2, j))
+
+    def arrive(self, j):
+        wait(self.hand(0, j))
+        wait(self.hand(2, j))
+        start(self.save0(j))
+
+    def leave(self):
+        for j in range(J):
+            wait(self.save0(j))
+        wait(self.own1())
+        wait(self.y1())
+        start(self.p2())
+        wait(self.p1())
+        wait(self.p2())
+
+
+def start(copies):
     for copy in copies:
         copy.start()
+
+
+def wait(copies):
+    for copy in copies:
+        copy.wait()
+
+
+def rows(ref, *index):
+    got = ref[index]
+    return got.reshape(-1, got.shape[-1])
+
+
+def fwd_kernel(h_hbm, wg_hbm, wu_hbm, wd_hbm, o_hbm, *refs):
+    outs, (h_v, a_v, yT_v, wgu_v, wd_v, wdT_v, s_v, owngu, ownd, hsem, *sems) = refs[:4], refs[4:]
+    gather = Gather((wg_hbm, wu_hbm, wd_hbm), outs, (wgu_v, wd_v), (owngu, ownd), *sems)
+    load = pltpu.make_async_copy(h_hbm, h_v, hsem)
+    mine = gather.mine(0)
+    start(mine)
+    start(gather.mine(1))
+    load.start()
+    gather.enter()
+    wait(mine)
+    start(gather.hand(1, 0))
+    start(gather.hand(0, 0))
+    wait(gather.mine(1))
+    start(gather.x1())
+    for j in range(1, J):
+        start(gather.hand(1, j))
+        start(gather.hand(0, j))
+    start(gather.own1())
     yT_v[...] = jnp.zeros_like(yT_v)
     s_v[1] = jnp.zeros_like(s_v[1])
-    copies[0].wait()
+    wdT_v[...] = jnp.zeros_like(wdT_v)
+    load.wait()
 
     @pl.loop(0, NB)
     def _(t):
         wide = h_v[t].astype(f32)
         a_v[t] = (wide * scale_of(wide)).astype(bf16)
 
-    for copy in copies[1:]:
-        copy.wait()
-
-    @pl.loop(0, J)
-    def _(j):
-        wdT_v[j] = wd_v[j].T
+    wait(gather.hand(1, 0))
+    start(gather.hand(2, 0))
 
     def front(j, t):
-        return dot(a_v[t], wg_v[j]), dot(a_v[t], wu_v[j])
+        return dot(a_v[t], rows(wgu_v, 0, j)), dot(a_v[t], rows(wgu_v, 1, j))
 
     def mid(gate, up):
         return (gate * jax.nn.sigmoid(gate) * up).astype(bf16)
@@ -66,6 +207,16 @@
     @pl.loop(0, STEPS // 2)
     def _(pair):
         i = 2 * pair
+        for j in range(J):
+
+            @pl.when(i == NB * j)
+            def _():
+                gather.arrive(j)
+
+        @pl.when(i % NB == 0)
+        def _():
+            wdT_v[i // NB] = rows(wd_v, i // NB).T
+
         before = jnp.maximum(i - 1, 0)
         first = front(i // NB, i % NB)
         back(before // NB, before % NB, s_v[1])
@@ -73,6 +224,7 @@
         second = front((i + 1) // NB, (i + 1) % NB)
         back(i // NB, i % NB, s_v[0])
         s_v[1] = mid(*second)
+        gather.tick(i)
 
     back(J - 1, NB - 1, s_v[1])
 
@@ -80,34 +232,44 @@
     def _(t):
         h_v[t] = h_v[t] + yT_v[t].astype(bf16).T
 
-    copy = pltpu.make_async_copy(h_v, o_hbm, osem)
+    copy = pltpu.make_async_copy(h_v, o_hbm, hsem)
     copy.start()
+    gather.leave()
     copy.wait()
 
 
-def forward(h, wg, wu, wd):
+def forward(h, *weights):
     anywhere = pl.BlockSpec(memory_space=pl.ANY)
+    shapes = [jax.ShapeDtypeStruct(s, bf16) for s in (GATE_UP, DOWN)]
+    dma = pltpu.SemaphoreType.DMA
     return pl.pallas_call(
         fwd_kernel,
-        out_shape=jax.ShapeDtypeStruct((NB, TB, D), bf16),
+        out_shape=(jax.ShapeDtypeStruct((NB, TB, D), bf16), *shapes, *shapes),
         in_specs=[anywhere] * 4,
-        out_specs=anywhere,
+        out_specs=(anywhere,) * 5,
         scratch_shapes=[
             pltpu.VMEM((NB, TB, D), bf16),
             pltpu.VMEM((NB, TB, D), bf16),
             pltpu.VMEM((NB, D, TB), f32),
-            pltpu.VMEM((J, D, FC), bf16),
-            pltpu.VMEM((J, D, FC), bf16),
-            pltpu.VMEM((J, FC, D), bf16),
+            pltpu.VMEM(GATE_UP, bf16),
+            pltpu.VMEM(DOWN, bf16),
             pltpu.VMEM((J, D, FC), bf16),
             pltpu.VMEM((2, TB, FC), bf16),
-            pltpu.SemaphoreType.DMA((4,)),
-            pltpu.SemaphoreType.DMA,
+            pltpu.VMEM((2, J, 2, HR, FC), bf16),
+            pltpu.VMEM((J, 2, DR, D), bf16),
+            dma,
+            dma((2, 18 * J)),
+            dma((J, 2)),
+            dma((2,)),
+            dma((3, J, 2, 2)),
+            dma((2, 2)),
+            dma((ZS - 1, 2, 2)),
+            dma((8, 2)),
         ],
-        compiler_params=pltpu.CompilerParams(vmem_limit_bytes=VMEM_LIMIT),
+        compiler_params=pltpu.CompilerParams(vmem_limit_bytes=VMEM_LIMIT, collective_id=0, has_side_effects=True),
         cost_estimate=pl.CostEstimate(flops=6 * T * D * F, bytes_accessed=20_000_000, transcendentals=0),
-        name="forward",
-    )(h, wg, wu, wd)
+        name="forward_gather",
+    )(h, *weights)
 
 
 class Reduction:
@@ -257,13 +419,13 @@
 
 
 def bwd_kernel(reduce, *refs):
-    h_hbm, dy_hbm, wg_hbm, wu_hbm, wd_hbm, *refs = refs
+    h_hbm, dy_hbm, wgu_hbm, wd_hbm, *refs = refs
     g1_hbm, dh_hbm, g_hbm, *refs = refs if reduce else (None, *refs)
     out_hbm, *refs = refs if reduce else (None, *refs)
-    dy_v, a_v, aT_v, dyT_v, daT_v, wg_v, wu_v, wd_v, acc_v, gb_v, s_v, sem, gsem, hsem, *refs = refs
+    dy_v, a_v, aT_v, dyT_v, daT_v, wgu_v, wd_v, acc_v, gb_v, s_v, sem, gsem, hsem, *refs = refs
     copies = [
         pltpu.make_async_copy(src, dst, sem.at[i])
-        for i, (src, dst) in enumerate([(h_hbm, a_v), (dy_hbm, dy_v), (wg_hbm, wg_v), (wu_hbm, wu_v), (wd_hbm, wd_v)])
+        for i, (src, dst) in enumerate([(h_hbm, a_v), (dy_hbm, dy_v), (wgu_hbm, wgu_v), (wd_hbm, wd_v)])
     ]
     for copy in copies:
         copy.start()
@@ -290,7 +452,7 @@
         copy.wait()
 
     def front(j, t):
-        return dot(a_v[t], wg_v[j]), dot(a_v[t], wu_v[j]), dot_nt(dy_v[t], wd_v[j])
+        return dot(a_v[t], rows(wgu_v, 0, j)), dot(a_v[t], rows(wgu_v, 1, j)), dot_nt(dy_v[t], rows(wd_v, j))
 
     def mid(slot, gate, up, dact):
         dact = dact.astype(bf16).astype(f32)
@@ -302,7 +464,7 @@
 
     def back(j, t, slot):
         act, dgate, dup = s_v[slot, 0], s_v[slot, 1], s_v[slot, 2]
-        daT_v[t] += dot_nt(wg_v[j], dgate) + dot_nt(wu_v[j], dup)
+        daT_v[t] += dot_nt(rows(wgu_v, 0, j), dgate) + dot_nt(rows(wgu_v, 1, j), dup)
         acc_v[0] += dot(aT_v[t], dgate)
         acc_v[1] += dot(aT_v[t], dup)
         acc_v[2] += dot(dyT_v[t], act)
@@ -382,7 +544,7 @@
     copy.wait()
 
 
-def backward(h, dy, wg, wu, wd, g1=None):
+def backward(h, dy, wgu, wd, g1=None):
     reduce = g1 is not None
     anywhere = pl.BlockSpec(memory_space=pl.ANY)
     tokens, turned, grads = (NB, TB, D), (NB, D, TB), (J, 3, CS, XS, 2, 4, HR, QL)
@@ -393,13 +555,12 @@
         pltpu.VMEM(turned, bf16),
         pltpu.VMEM(turned, bf16),
         pltpu.VMEM(turned, f32),
-        pltpu.VMEM((J, D, FC), bf16),
-        pltpu.VMEM((J, D, FC), bf16),
-        pltpu.VMEM((J, FC, D), bf16),
+        pltpu.VMEM(GATE_UP, bf16),
+        pltpu.VMEM(DOWN, bf16),
         pltpu.VMEM((3, D, FC), f32),
         pltpu.VMEM(grads[1:], bf16),
         pltpu.VMEM((2, 3, TB, FC), bf16),
-        pltpu.SemaphoreType.DMA((5,)),
+        pltpu.SemaphoreType.DMA((4,)),
         pltpu.SemaphoreType.DMA,
         pltpu.SemaphoreType.DMA,
     ]
@@ -429,7 +590,7 @@
             pltpu.SemaphoreType.DMA,
             pltpu.SemaphoreType.REGULAR((6,)),
         ]
-    args = (h, dy, wg, wu, wd) + ((g1,) if reduce else ())
+    args = (h, dy, wgu, wd) + ((g1,) if reduce else ())
     return pl.pallas_call(
         lambda *refs: bwd_kernel(reduce, *refs),
         out_shape=tuple(outs),
@@ -446,16 +607,10 @@
 
 def solution(mesh):
     def step(x, dy, *weights):
-        def fetched(l):
-            wg, wu, wd = [lax.all_gather(w[l], "s", axis=0, tiled=True) for w in weights]
-            cols = [w.reshape(D, 4, J, QL).transpose(2, 0, 1, 3).reshape(J, D, FC) for w in (wg, wu)]
-            return (*cols, wd.reshape(4, J, QL, D).transpose(1, 0, 2, 3).reshape(J, FC, D))
-
-        w0, w1 = fetched(0), fetched(1)
         h0, dy = x.reshape(NB, TB, D), dy.reshape(NB, TB, D)
-        h1 = forward(h0, *w0)
-        dh1, g1 = backward(h1, dy, *w1)
-        dx, _, total = backward(h0, dh1, *w0, g1)
+        h1, gate_up0, down0, gate_up1, down1 = forward(h0, *weights)
+        dh1, g1 = backward(h1, dy, gate_up1, down1)
+        dx, _, total = backward(h0, dh1, gate_up0, down0, g1)
         total = total.reshape(2, J, 3, 2, 4, HR, QL)[::-1]
         cols = [total[:, :, m].transpose(0, 2, 4, 3, 1, 5).reshape(2, 2 * HR, F) for m in range(2)]
         down = total[:, :, 2].transpose(0, 1, 5, 3, 2, 4).reshape(2, F // 4, D)

time: 553 us -> 391 us (0.71); the launches traced: 543 us -> 391 us
  waiting for transfers between devices: 109 us -> 0 us
  local copies, waits for them, and re-layouts: 80.8 us -> 20.9 us
  Pallas kernels: 338 us -> 369 us
  between operations: 14.7 us -> 0.69 us
    all_gather x6 -> x0, waiting for transfers between devices: 107 us -> none  [fetched(): lax.all_gather(w[l], 's', axis=0, tiled=True)]
    reshape x14 -> x0, local copies, waits for them, and re-layouts: 54.7 us -> none  [the longest x12 47.5 us: fetched(): w.reshape(D, 4, J, QL).transpose(2, 0, 1, 3).reshape(J, D, FC)]
    pallas_call x1, Pallas kernels: 50.1 us -> 82.4 us  [forward(): pl.pallas_call(fwd_kernel, out_shape=(jax.ShapeDtypeStruct((NB, TB, D), b...]
  transfers between devices with their start and end apart: 6 -> 0, of which waited for: 6 -> 0; matrix products, arithmetic and copies ran while one was open for 10% -> 0% of each run, Pallas kernels for 0% -> 0%
where the time goes in v2:
time: 391 us
  Pallas kernels  369 us (94%)
  local copies, waits for them, and re-layouts  20.9 us (5%)
    pallas_call x2, Pallas kernels, backward(): pl.pallas_call(lambda *refs: bwd_kernel(reduce, *refs), out_shape=tuple(o...  287 us
    pallas_call x1, Pallas kernels, forward(): pl.pallas_call(fwd_kernel, out_shape=(jax.ShapeDtypeStruct((NB, TB, D), b...  82.4 us

profile of v2, /device:TPU:0, one launch (start us, length us, event | category | flops | bytes accessed | tf_op | source)
XLA Modules:
  0.0 390.9 jit_solution(5149804894736513618)
XLA Ops:
  0.6 82.4 %forward_gather.1 = (bf16[8,512,640]{2,1,0:T(8,128)(2,1)}, bf16[2,4,4,2,80,512]{5,4,3,2,1,0:T(8,128)(2,1)}, bf16[4,4,2,64,640]{4,3,2,1,0:T(8,128)(2,1)}, bf16[2,...) custom-call(bf16[8,512,640]{2,1,0:T(8,128)(2,1)} %bitcast.21, bf16[2,160,2048]{2,1,0:T(8,128)(2,1)} %wg_hbm.1, ...), custom_call_target="tpu_custom_call" | custom-call | flops 32212254720 | bytes 20000000 | tf_op jit(solution)/shard_map/forward_gather/pallas_call | solution.py:245
  83.1 124.3 %backward.1 = (bf16[8,512,640]{2,1,0:T(8,128)(2,1)}, bf16[4,3,2,2,2,4,80,128]{7,6,5,4,3,2,1,0:T(8,128)(2,1)}) custom-call(bf16[8,512,640]{2,1,0:T(8,128)(2,1)} %get-tuple-element.13.refs_0_, bf16[8,512,640]{2,1,0:T(8,128)(2,1)} %bitcast.20, bf16[2,4,4,2,80,512]{5,4,3,2,1,0:T(8,128)(2,1)} %get-tuple-element.14.refs_2_, ...), custom_call_target="tpu_custom_call" | custom-call | flops 85899345920 | bytes 30000000 | tf_op jit(solution)/shard_map/backward/pallas_call | solution.py:594
  207.4 162.6 %backward_reduce.1 = (bf16[8,512,640]{2,1,0:T(8,128)(2,1)}, bf16[4,3,2,2,2,4,80,128]{7,6,5,4,3,2,1,0:T(8,128)(2,1)}, bf16[8,3,2,4,80,128]{5,4,3,2,1,0:T(8,128)(2,1)}) custom-call(bf16[8,512,640]{2,1,0:T(8,128)(2,1)} %bitcast.22, bf16[8,512,640]{2,1,0:T(8,128)(2,1)} %get-tuple-element.16.refs_1_, bf16[2,4,4,2,80,512]{5,4,3,2,1,0:T(8,128)(2,1)} %get-tuple-element.17.refs_2_, ...), custom_call_target="tpu_custom_call" | custom-call | flops 85899345920 | bytes 30000000 | tf_op jit(solution)/shard_map/backward_reduce/pallas_call | solution.py:594
  370.0 4.5 %fusion = (bf16[2,4,1,2,4,80,128]{6,5,4,3,2,1,0:T(8,128)(2,1)S(1)}, bf16[2,4,1,2,4,80,128]{6,5,4,3,2,1,0:T(8,128)(2,1)}, bf16[2,4,1,2,4,80,128]{6,5,4,3,2,1,0:T(8,128)(2,1)}) fusion(bf16[2,4,3,2,4,80,128]{6,5,4,3,2,1,0:T(8,128)(2,1)} %bitcast.19), kind=kLoop, calls=%fused_computation.3 | loop fusion | bytes 7864320 | tf_op jit(solution)/shard_map/slice | solution.py:616
  374.5 1.0 copy.16
  375.5 0.5 reverse_bitcast_fusion
  376.0 0.5 reshape.35
  376.6 1.4 copy.15
  378.0 1.9 reverse_bitcast_fusion.1
  379.9 1.0 copy.13
  381.0 1.8 reshape.34
  382.8 1.0 copy.12
  383.8 1.8 reshape.33
  385.6 5.3 %copy.18 = bf16[1,4096,640]{2,1,0:T(8,128)(2,1)} copy(bf16[1,4096,640]{2,1,0:T(8,128)(2,1)} %bitcast.18) | data formatting | bytes 10485760

commit v3 on v2

--- a/solution.py
+++ b/solution.py
@@ -13,7 +13,7 @@
 HR, DR, QL = D // 8, FC // 8, FC // 4
 GATE_UP, DOWN = (2, J, 4, 2, HR, FC), (J, 4, 2, DR, D)
 SLOTS = 6
-TICKS = 46
+DEEP, AHEAD = 4, 2
 VMEM_LIMIT = 67_000_000
 bf16, f32 = jnp.bfloat16, jnp.float32
 NT = (((1,), (1,)), ((), ()))
@@ -159,19 +159,22 @@
         copy.wait()
 
 
+def block(src, dst, t, sems):
+    return pltpu.make_async_copy(src.at[t], dst.at[t], sems.at[t])
+
+
 def rows(ref, *index):
     got = ref[index]
     return got.reshape(-1, got.shape[-1])
 
 
 def fwd_kernel(h_hbm, wg_hbm, wu_hbm, wd_hbm, o_hbm, *refs):
-    outs, (h_v, a_v, yT_v, wgu_v, wd_v, wdT_v, s_v, owngu, ownd, hsem, *sems) = refs[:4], refs[4:]
+    outs, gu_hbm, (h_v, a_v, yT_v, wgu_v, wd_v, wdT_v, s_v, gu_v, owngu, ownd, hsem, gsem, *sems) = refs[:4], refs[4], refs[5:]
     gather = Gather((wg_hbm, wu_hbm, wd_hbm), outs, (wgu_v, wd_v), (owngu, ownd), *sems)
-    load = pltpu.make_async_copy(h_hbm, h_v, hsem)
     mine = gather.mine(0)
     start(mine)
     start(gather.mine(1))
-    load.start()
+    start([block(h_hbm, h_v, t, hsem) for t in range(NB)])
     gather.enter()
     wait(mine)
     start(gather.hand(1, 0))
@@ -185,10 +188,10 @@
     yT_v[...] = jnp.zeros_like(yT_v)
     s_v[1] = jnp.zeros_like(s_v[1])
     wdT_v[...] = jnp.zeros_like(wdT_v)
-    load.wait()
 
     @pl.loop(0, NB)
     def _(t):
+        block(h_hbm, h_v, t, hsem).wait()
         wide = h_v[t].astype(f32)
         a_v[t] = (wide * scale_of(wide)).astype(bf16)
 
@@ -198,8 +201,13 @@
     def front(j, t):
         return dot(a_v[t], rows(wgu_v, 0, j)), dot(a_v[t], rows(wgu_v, 1, j))
 
-    def mid(gate, up):
-        return (gate * jax.nn.sigmoid(gate) * up).astype(bf16)
+    def mid(i, slot, gate, up):
+        gu_v[i % DEEP, 0] = gate
+        gu_v[i % DEEP, 1] = up
+        s_v[slot] = (gate * jax.nn.sigmoid(gate) * up).astype(bf16)
+
+    def save(i):
+        return pltpu.make_async_copy(gu_v.at[i % DEEP], gu_hbm.at[i], gsem.at[i % DEEP])
 
     def back(j, t, act):
         yT_v[t] += dot_nt(wdT_v[j], act)
@@ -217,13 +225,18 @@
         def _():
             wdT_v[i // NB] = rows(wd_v, i // NB).T
 
+        @pl.when(i >= DEEP)
+        def _():
+            wait([save(i - DEEP), save(i + 1 - DEEP)])
+
         before = jnp.maximum(i - 1, 0)
         first = front(i // NB, i % NB)
         back(before // NB, before % NB, s_v[1])
-        s_v[0] = mid(*first)
+        mid(i, 0, *first)
         second = front((i + 1) // NB, (i + 1) % NB)
         back(i // NB, i % NB, s_v[0])
-        s_v[1] = mid(*second)
+        mid(i + 1, 1, *second)
+        start([save(i), save(i + 1)])
         gather.tick(i)
 
     back(J - 1, NB - 1, s_v[1])
@@ -231,11 +244,11 @@
     @pl.loop(0, NB)
     def _(t):
         h_v[t] = h_v[t] + yT_v[t].astype(bf16).T
-
-    copy = pltpu.make_async_copy(h_v, o_hbm, hsem)
-    copy.start()
+        block(h_v, o_hbm, t, hsem).start()
+
     gather.leave()
-    copy.wait()
+    wait([block(h_v, o_hbm, t, hsem) for t in range(NB)])
+    wait([save(i) for i in range(STEPS - DEEP, STEPS)])
 
 
 def forward(h, *weights):
@@ -244,9 +257,9 @@
     dma = pltpu.SemaphoreType.DMA
     return pl.pallas_call(
         fwd_kernel,
-        out_shape=(jax.ShapeDtypeStruct((NB, TB, D), bf16), *shapes, *shapes),
+        out_shape=(jax.ShapeDtypeStruct((NB, TB, D), bf16), *shapes, *shapes, jax.ShapeDtypeStruct((STEPS, 2, TB, FC), f32)),
         in_specs=[anywhere] * 4,
-        out_specs=(anywhere,) * 5,
+        out_specs=(anywhere,) * 6,
         scratch_shapes=[
             pltpu.VMEM((NB, TB, D), bf16),
             pltpu.VMEM((NB, TB, D), bf16),
@@ -255,9 +268,11 @@
             pltpu.VMEM(DOWN, bf16),
             pltpu.VMEM((J, D, FC), bf16),
             pltpu.VMEM((2, TB, FC), bf16),
+            pltpu.VMEM((DEEP, 2, TB, FC), f32),
             pltpu.VMEM((2, J, 2, HR, FC), bf16),
             pltpu.VMEM((J, 2, DR, D), bf16),
-            dma,
+            dma((NB,)),
+            dma((DEEP,)),
             dma((2, 18 * J)),
             dma((J, 2)),
             dma((2,)),
@@ -273,7 +288,7 @@
 
 
 class Reduction:
-    def __init__(self, g1_hbm, g0_hbm, out_hbm, gbuf, drecv, xs, xrecv, ys, yrecv, keep, zs, zrecv, fq, dsem, xsem, ysem, zsem, fsem, asem, lsem, psem, near):
+    def __init__(self, groups, spread, delays, out_hbm, gbuf, drecv, xs, xrecv, ys, yrecv, keep, zs, zrecv, fq, dsem, xsem, ysem, zsem, fsem, asem, lsem, near):
         self.__dict__.update({k: v for k, v in locals().items() if k != "self"})
         r, s = lax.axis_index("r"), lax.axis_index("s")
         self.y, self.z, self.x, self.c = r // ZS, r % ZS, s // CS, s % CS
@@ -289,15 +304,8 @@
             pl.semaphore_signal(barrier, inc=1, device_id=peer, device_id_type=MESH)
         pl.semaphore_wait(barrier, len(self.peers))
 
-    def load(self, g):
-        return pltpu.make_async_copy(self.g1_hbm.at[g], self.gbuf.at[g % 2], self.psem)
-
-    def load0(self, g):
-        return pltpu.make_async_copy(self.g0_hbm.at[g - J], self.gbuf.at[g % 2], self.psem)
-
     def at(self, k):
-        block = k // 4
-        return (k >= 0) & (k % 4 < 3) & (block != 6) & (block < 9), block - jnp.where(block > 6, 1, 0), k % 4
+        return (k >= 0) & (k % 8 < 3 * self.spread) & (k % self.spread == 0) & (k < 8 * self.groups), k // 8, k % 8 // self.spread
 
     def remote(self, src, dst, sems, peer):
         return pltpu.make_async_remote_copy(src, dst, sems.at[0], sems.at[1], device_id=peer, device_id_type=MESH)
@@ -329,28 +337,16 @@
 
         @pl.when(valid)
         def _():
-            body(g, m, (k - delay) % SLOTS)
+            body(g, m, g % 2 * 3 + m)
 
     def tick(self, k):
         x, c, y, z = self.x, self.c, self.y, self.z
         gbuf, drecv, xrecv, keep = self.gbuf, self.drecv, self.xrecv, self.keep
 
-        @pl.when(k >= 2)
+        @pl.when((k % 8 == 0) & (k >= 16) & (k < 8 * self.groups))
         def _():
             for i in range(len(self.peers)):
                 pl.semaphore_wait(self.near.at[i], 1)
-
-        ahead = k + 2
-        block = ahead // 4
-        turn = (ahead % 4 == 0) & (k >= 0)
-
-        @pl.when(turn & (block < J))
-        def _():
-            self.load(block).start()
-
-        @pl.when(turn & (block >= J) & (block < 8) & (block != 6))
-        def _():
-            self.load0(block - jnp.where(block > 6, 1, 0)).start()
 
         def end(g, m, slot):
             self.acopy(g, m, slot).wait()
@@ -382,236 +378,282 @@
             self.xcopy(slot).wait()
 
             def total(half):
-                return gbuf[g % 2, m, c, x, half].astype(f32) + drecv[slot, x, half].astype(f32) + xrecv[slot, half].astype(f32)
+                return gbuf[g % self.spread, m, c, x, half].astype(f32) + drecv[slot, x, half].astype(f32) + xrecv[slot, half].astype(f32)
 
             self.ys[slot] = total(1 - y).astype(bf16)
             self.ycopy(slot).start()
             keep[slot] = total(y)
 
         def to_x(g, m, slot):
-            self.dcopy(g % 2, m, slot).wait()
-            self.xs[slot] = (gbuf[g % 2, m, c, 1 - x].astype(f32) + drecv[slot, 1 - x].astype(f32)).astype(bf16)
+            self.dcopy(g % self.spread, m, slot).wait()
+            self.xs[slot] = (gbuf[g % self.spread, m, c, 1 - x].astype(f32) + drecv[slot, 1 - x].astype(f32)).astype(bf16)
             self.xcopy(slot).start()
 
         def to_partner(g, m, slot):
-            @pl.when((m == 0) & (g < J))
-            def _():
-                self.load(g).wait()
-
-            @pl.when((m == 0) & (g >= J) & (g < 2 * J - 1))
-            def _():
-                self.load0(g).wait()
-
-            self.dcopy(g % 2, m, slot).start()
-
-        self.stage(k, 11, end)
-        self.stage(k, 9, gather_y)
-        self.stage(k, 7, finish)
-        self.stage(k, 5, to_z)
-        self.stage(k, 3, to_y)
-        self.stage(k, 1, to_x)
-        self.stage(k, 0, to_partner)
-
-        @pl.when(k < TICKS - 2)
+            self.dcopy(g % self.spread, m, slot).start()
+
+        for delay, body in zip(self.delays, (end, gather_y, finish, to_z, to_y, to_x, to_partner), strict=True):
+            self.stage(k, delay, body)
+        done = 2 * self.spread + self.delays[2]
+
+        @pl.when((k >= done) & ((k - done) % 8 == 0) & (k - done < 8 * (self.groups - 2)))
         def _():
             for i, peer in enumerate(self.peers):
                 pl.semaphore_signal(self.near.at[i], inc=1, device_id=peer, device_id_type=MESH)
 
 
-def bwd_kernel(reduce, *refs):
+def bwd_kernel(last, *refs):
     h_hbm, dy_hbm, wgu_hbm, wd_hbm, *refs = refs
-    g1_hbm, dh_hbm, g_hbm, *refs = refs if reduce else (None, *refs)
-    out_hbm, *refs = refs if reduce else (None, *refs)
-    dy_v, a_v, aT_v, dyT_v, daT_v, wgu_v, wd_v, acc_v, gb_v, s_v, sem, gsem, hsem, *refs = refs
-    copies = [
-        pltpu.make_async_copy(src, dst, sem.at[i])
-        for i, (src, dst) in enumerate([(h_hbm, a_v), (dy_hbm, dy_v), (wgu_hbm, wgu_v), (wd_hbm, wd_v)])
-    ]
-    for copy in copies:
-        copy.start()
-    red = None
-    if reduce:
-        red = Reduction(g1_hbm, g_hbm, out_hbm, *refs)
-        red.load(0).start()
-        red.enter()
+    if last:
+        g_hbm, gu_hbm, dh_hbm, ds_hbm, out_hbm, *refs = refs
+    else:
+        dh_hbm, g_hbm, out_hbm, *refs = refs
+    dy_v, h_v, aT_v, dyT_v, wgu_v, wd_v, acc_v, s_v, hsem, ysem, wsem, gsem, *refs = refs
+    if last:
+        daT_v, gu_v, ds_v, usem, dsem, esem, *refs = refs
+    else:
+        daT_v, a_v, *refs = refs
+    plan = (J + 1, 2, (18, 14, 10, 6, 4, 1, 0)) if last else (J - 1, 1, (11, 9, 7, 5, 3, 1, 0))
+    red = Reduction(*plan, out_hbm, *refs)
+
+    def weights(j):
+        return [pltpu.make_async_copy(wgu_hbm.at[:, j], wgu_v.at[:, j], wsem.at[j, 0]), pltpu.make_async_copy(wd_hbm.at[j], wd_v.at[j], wsem.at[j, 1])]
+
+    def saved(i):
+        return pltpu.make_async_copy(gu_hbm.at[i], gu_v.at[i % AHEAD], usem.at[i % AHEAD])
+
+    def spill(i, slot):
+        return pltpu.make_async_copy(s_v.at[slot, pl.ds(1, 2)], ds_hbm.at[i // NB, i % NB], dsem.at[slot])
+
+    def fetch(t, slot):
+        return pltpu.make_async_copy(ds_hbm.at[:, t], ds_v.at[slot], esem.at[slot])
+
+    for t in range(NB):
+        start([block(h_hbm, h_v, t, hsem), block(dy_hbm, dy_v, t, ysem)])
+    for j in range(J):
+        start(weights(j))
+    if last:
+        first_group = pltpu.make_async_copy(g_hbm, red.gbuf.at[0], gsem)
+        start([first_group, *(saved(i) for i in range(AHEAD))])
+    red.enter()
     acc_v[...] = jnp.zeros_like(acc_v)
-    daT_v[...] = jnp.zeros_like(daT_v)
     s_v[1] = jnp.zeros_like(s_v[1])
-    copies[0].wait()
-    copies[1].wait()
+    if not last:
+        daT_v[...] = jnp.zeros_like(daT_v)
 
     @pl.loop(0, NB)
     def _(t):
-        wide = a_v[t].astype(f32)
+        wait([block(h_hbm, h_v, t, hsem), block(dy_hbm, dy_v, t, ysem)])
+        wide = h_v[t].astype(f32)
         a = (wide * scale_of(wide)).astype(bf16)
-        a_v[t] = a
+        if not last:
+            a_v[t] = a
         aT_v[t] = a.T
         dyT_v[t] = dy_v[t].T
 
-    for copy in copies[2:]:
-        copy.wait()
+    if last:
+        first_group.wait()
 
     def front(j, t):
-        return dot(a_v[t], rows(wgu_v, 0, j)), dot(a_v[t], rows(wgu_v, 1, j)), dot_nt(dy_v[t], rows(wd_v, j))
-
-    def mid(slot, gate, up, dact):
+        dact = dot_nt(dy_v[t], rows(wd_v, j))
+        if last:
+            return (dact,)
+        return dact, dot(a_v[t], rows(wgu_v, 0, j)), dot(a_v[t], rows(wgu_v, 1, j))
+
+    def mid(i, slot, dact, gate=None, up=None):
+        if last:
+            gate, up = gu_v[i % AHEAD, 0], gu_v[i % AHEAD, 1]
         dact = dact.astype(bf16).astype(f32)
         sg = jax.nn.sigmoid(gate)
         s = gate * sg
         s_v[slot, 0] = (s * up).astype(bf16)
         s_v[slot, 1] = (dact * up * (sg + s * (1.0 - sg))).astype(bf16)
         s_v[slot, 2] = (dact * s).astype(bf16)
+        if last:
+            spill(i, slot).start()
+
+            @pl.when(i + AHEAD < STEPS)
+            def _():
+                saved(i + AHEAD).start()
 
     def back(j, t, slot):
         act, dgate, dup = s_v[slot, 0], s_v[slot, 1], s_v[slot, 2]
-        daT_v[t] += dot_nt(rows(wgu_v, 0, j), dgate) + dot_nt(rows(wgu_v, 1, j), dup)
+        if not last:
+            daT_v[t] += dot_nt(rows(wgu_v, 0, j), dgate) + dot_nt(rows(wgu_v, 1, j), dup)
         acc_v[0] += dot(aT_v[t], dgate)
         acc_v[1] += dot(aT_v[t], dup)
         acc_v[2] += dot(dyT_v[t], act)
 
-    def flush(dst):
+    def flush(b):
         for x in range(XS):
             for c in range(CS):
                 n = x * CS + c
                 for h in range(2):
                     for q in range(4):
-                        rows = slice(n * 2 * HR + h * HR, n * 2 * HR + (h + 1) * HR)
+                        part = slice(n * 2 * HR + h * HR, n * 2 * HR + (h + 1) * HR)
                         for m in range(2):
-                            dst[m, c, x, h, q] = acc_v[m, rows, q * QL : (q + 1) * QL].astype(bf16)
-                        rows = slice(q * 2 * HR + h * HR, q * 2 * HR + (h + 1) * HR)
-                        dst[2, c, x, h, q] = acc_v[2, rows, n * QL : (n + 1) * QL].astype(bf16)
-
-    def put(j):
-        return pltpu.make_async_copy(gb_v, g_hbm.at[j], gsem)
+                            red.gbuf[b, m, c, x, h, q] = acc_v[m, part, q * QL : (q + 1) * QL].astype(bf16)
+                        part = slice(q * 2 * HR + h * HR, q * 2 * HR + (h + 1) * HR)
+                        red.gbuf[b, 2, c, x, h, q] = acc_v[2, part, n * QL : (n + 1) * QL].astype(bf16)
+
+    def tick(i):
+        if last:
+            red.tick(i)
+        else:
+
+            @pl.when(i >= NB)
+            def _():
+                red.tick(i - NB)
+
+    def norm_back(t, da):
+        da = da.astype(bf16).T.astype(f32)
+        wide = h_v[t].astype(f32)
+        scale = scale_of(wide)
+        mean = jnp.mean(da * wide, -1, keepdims=True)
+        dy_v[t] = dy_v[t] + (da * scale - wide * (scale * scale * scale * mean)).astype(bf16)
+        block(dy_v, dh_hbm, t, hsem).start()
 
     @pl.loop(0, STEPS // 2)
     def _(pair):
         i = 2 * pair
+
+        @pl.when(i % NB == 0)
+        def _():
+            wait(weights(i // NB))
+
         before = jnp.maximum(i - 1, 0)
+        if last:
+
+            @pl.when(pair > 0)
+            def _():
+                spill(i - 2, 0).wait()
+
+            saved(i).wait()
         first = front(i // NB, i % NB)
         back(before // NB, before % NB, 1)
-        mid(0, *first)
+        mid(i, 0, *first)
 
         @pl.when((i % NB == 0) & (pair > 0))
         def _():
-            flush(gb_v)
-            put(before // NB).start()
+            flush(i // NB % red.spread)
             acc_v[...] = jnp.zeros_like(acc_v)
 
-        if reduce:
-            red.tick(i)
+        tick(i)
+        if last:
+
+            @pl.when(pair > 0)
+            def _():
+                spill(i - 1, 1).wait()
+
+            saved(i + 1).wait()
         second = front((i + 1) // NB, (i + 1) % NB)
         back(i // NB, i % NB, 0)
-        mid(1, *second)
-
-        @pl.when((i % NB == 0) & (pair > 0))
-        def _():
-            put(before // NB).wait()
-
-        if reduce:
-            red.tick(i + 1)
-
-    reload = pltpu.make_async_copy(h_hbm, a_v, hsem)
-    reload.start()
+        mid(i + 1, 1, *second)
+        tick(i + 1)
+
+    if last:
+        wait([spill(STEPS - 2, 0), spill(STEPS - 1, 1)])
+        start([fetch(0, 0), fetch(1, 1)])
     back(J - 1, NB - 1, 1)
-    if reduce:
-        flush(red.gbuf.at[1])
-    else:
-        flush(gb_v)
-        put(J - 1).start()
-    reload.wait()
-
-    @pl.loop(0, NB)
-    def _(t):
-        if reduce:
-            red.tick(STEPS + t)
-        da = daT_v[t].astype(bf16).T.astype(f32)
-        wide = a_v[t].astype(f32)
-        scale = scale_of(wide)
-        mean = jnp.mean(da * wide, -1, keepdims=True)
-        dy_v[t] = dy_v[t] + (da * scale - wide * (scale * scale * scale * mean)).astype(bf16)
-
-    copy = pltpu.make_async_copy(dy_v, dh_hbm, hsem)
-    copy.start()
-    if reduce:
-
-        @pl.loop(STEPS + NB, TICKS)
+    flush(0)
+    if last:
+
+        @pl.loop(0, NB)
+        def _(t):
+            slot = t % 2
+            fetch(t, slot).wait()
+            red.tick(STEPS + 2 * t)
+
+            def part(j):
+                return dot_nt(rows(wgu_v, 0, j), ds_v[slot, j, 0]) + dot_nt(rows(wgu_v, 1, j), ds_v[slot, j, 1])
+
+            daT_v[...] = part(0) + part(1)
+            red.tick(STEPS + 2 * t + 1)
+            norm_back(t, daT_v[...] + (part(2) + part(3)))
+
+            @pl.when(t + 2 < NB)
+            def _():
+                fetch(t + 2, slot).start()
+
+        @pl.loop(STEPS + 2 * NB, 8 * J + 4 + 19)
         def _(k):
             red.tick(k)
 
     else:
-        put(J - 1).wait()
-    copy.wait()
-
-
-def backward(h, dy, wgu, wd, g1=None):
-    reduce = g1 is not None
+        put = pltpu.make_async_copy(red.gbuf.at[0], g_hbm, gsem)
+        put.start()
+
+        @pl.loop(0, NB)
+        def _(t):
+            tick(STEPS + t)
+            norm_back(t, daT_v[t])
+
+        put.wait()
+    wait([block(dy_v, dh_hbm, t, hsem) for t in range(NB)])
+
+
+def backward(h, dy, wgu, wd, *more):
+    last = bool(more)
     anywhere = pl.BlockSpec(memory_space=pl.ANY)
-    tokens, turned, grads = (NB, TB, D), (NB, D, TB), (J, 3, CS, XS, 2, 4, HR, QL)
-    outs = [jax.ShapeDtypeStruct(tokens, bf16), jax.ShapeDtypeStruct(grads, bf16)]
-    scratch = [
-        pltpu.VMEM(tokens, bf16),
-        pltpu.VMEM(tokens, bf16),
-        pltpu.VMEM(turned, bf16),
-        pltpu.VMEM(turned, bf16),
-        pltpu.VMEM(turned, f32),
-        pltpu.VMEM(GATE_UP, bf16),
-        pltpu.VMEM(DOWN, bf16),
-        pltpu.VMEM((3, D, FC), f32),
-        pltpu.VMEM(grads[1:], bf16),
-        pltpu.VMEM((2, 3, TB, FC), bf16),
-        pltpu.SemaphoreType.DMA((4,)),
-        pltpu.SemaphoreType.DMA,
-        pltpu.SemaphoreType.DMA,
-    ]
-    if reduce:
-        piece = (2, 4, HR, QL)
-        outs.append(jax.ShapeDtypeStruct((2 * J, 3, *piece), bf16))
-        pair = pltpu.SemaphoreType.DMA((SLOTS, 2))
-        triple = pltpu.SemaphoreType.DMA((SLOTS, ZS - 1, 2))
-        scratch += [
-            pltpu.VMEM((2, *grads[1:]), bf16),
-            pltpu.VMEM((SLOTS, XS, *piece), bf16),
-            pltpu.VMEM((SLOTS, *piece), bf16),
-            pltpu.VMEM((SLOTS, *piece), bf16),
-            pltpu.VMEM((SLOTS, *piece[1:]), bf16),
-            pltpu.VMEM((SLOTS, *piece[1:]), bf16),
-            pltpu.VMEM((SLOTS, *piece[1:]), f32),
-            pltpu.VMEM((SLOTS, ZS - 1, *piece[2:]), bf16),
-            pltpu.VMEM((SLOTS, ZS - 1, *piece[2:]), bf16),
-            pltpu.VMEM((SLOTS, *piece[2:]), bf16),
-            pair,
-            pair,
-            pair,
-            triple,
-            triple,
-            pair,
-            pltpu.SemaphoreType.DMA((SLOTS,)),
-            pltpu.SemaphoreType.DMA,
+    tokens, turned, grads, piece = (NB, TB, D), (NB, D, TB), (3, CS, XS, 2, 4, HR, QL), (2, 4, HR, QL)
+    dma, vmem = pltpu.SemaphoreType.DMA, pltpu.VMEM
+    total = jax.ShapeDtypeStruct((J + 1 if last else J - 1, 3, *piece), bf16)
+    kept = jax.ShapeDtypeStruct((J, NB, 2, TB, FC) if last else grads, bf16)
+    if last:
+        own = [vmem((D, TB), f32), vmem((AHEAD, 2, TB, FC), f32), vmem((2, J, 2, TB, FC), bf16), dma((AHEAD,)), dma((2,)), dma((2,))]
+    else:
+        own = [vmem(turned, f32), vmem(tokens, bf16)]
+    return pl.pallas_call(
+        lambda *refs: bwd_kernel(last, *refs),
+        out_shape=(jax.ShapeDtypeStruct(tokens, bf16), kept, total),
+        in_specs=[anywhere] * (4 + len(more)),
+        out_specs=(anywhere,) * 3,
+        scratch_shapes=[
+            vmem(tokens, bf16),
+            vmem(tokens, bf16),
+            vmem(turned, bf16),
+            vmem(turned, bf16),
+            vmem(GATE_UP, bf16),
+            vmem(DOWN, bf16),
+            vmem((3, D, FC), f32),
+            vmem((2, 3, TB, FC), bf16),
+            dma((NB,)),
+            dma((NB,)),
+            dma((J, 2)),
+            dma,
+            *own,
+            vmem((2 if last else 1, *grads), bf16),
+            vmem((SLOTS, XS, *piece), bf16),
+            vmem((SLOTS, *piece), bf16),
+            vmem((SLOTS, *piece), bf16),
+            vmem((SLOTS, *piece[1:]), bf16),
+            vmem((SLOTS, *piece[1:]), bf16),
+            vmem((SLOTS, *piece[1:]), f32),
+            vmem((SLOTS, ZS - 1, *piece[2:]), bf16),
+            vmem((SLOTS, ZS - 1, *piece[2:]), bf16),
+            vmem((SLOTS, *piece[2:]), bf16),
+            dma((SLOTS, 2)),
+            dma((SLOTS, 2)),
+            dma((SLOTS, 2)),
+            dma((SLOTS, ZS - 1, 2)),
+            dma((SLOTS, ZS - 1, 2)),
+            dma((SLOTS, 2)),
+            dma((SLOTS,)),
             pltpu.SemaphoreType.REGULAR((6,)),
-        ]
-    args = (h, dy, wgu, wd) + ((g1,) if reduce else ())
-    return pl.pallas_call(
-        lambda *refs: bwd_kernel(reduce, *refs),
-        out_shape=tuple(outs),
-        in_specs=[anywhere] * len(args),
-        out_specs=(anywhere,) * len(outs),
-        scratch_shapes=scratch,
-        compiler_params=pltpu.CompilerParams(
-            vmem_limit_bytes=VMEM_LIMIT, **(dict(collective_id=1, has_side_effects=True) if reduce else {})
-        ),
-        cost_estimate=pl.CostEstimate(flops=16 * T * D * F, bytes_accessed=30_000_000, transcendentals=0),
-        name="backward_reduce" if reduce else "backward",
-    )(*args)
+        ],
+        compiler_params=pltpu.CompilerParams(vmem_limit_bytes=VMEM_LIMIT, collective_id=2 if last else 1, has_side_effects=True),
+        cost_estimate=pl.CostEstimate(flops=(12 if last else 16) * T * D * F, bytes_accessed=30_000_000, transcendentals=0),
+        name="backward_0" if last else "backward_1",
+    )(h, dy, wgu, wd, *more)
 
 
 def solution(mesh):
     def step(x, dy, *weights):
         h0, dy = x.reshape(NB, TB, D), dy.reshape(NB, TB, D)
-        h1, gate_up0, down0, gate_up1, down1 = forward(h0, *weights)
-        dh1, g1 = backward(h1, dy, gate_up1, down1)
-        dx, _, total = backward(h0, dh1, gate_up0, down0, g1)
-        total = total.reshape(2, J, 3, 2, 4, HR, QL)[::-1]
+        h1, gate_up0, down0, gate_up1, down1, saved = forward(h0, *weights)
+        dh1, left, total1 = backward(h1, dy, gate_up1, down1)
+        dx, _, total0 = backward(h0, dh1, gate_up0, down0, left, saved)
+        total = jnp.concatenate([total0[1:], total1, total0[:1]]).reshape(2, J, 3, 2, 4, HR, QL)
         cols = [total[:, :, m].transpose(0, 2, 4, 3, 1, 5).reshape(2, 2 * HR, F) for m in range(2)]
         down = total[:, :, 2].transpose(0, 1, 5, 3, 2, 4).reshape(2, F // 4, D)
         return dx.reshape(1, T, D), *cols, down

time: 391 us -> 360 us (0.921)
  Pallas kernels: 369 us -> 338 us
    pallas_call x2, Pallas kernels: 287 us -> 255 us  [backward(): pl.pallas_call(lambda *refs: bwd_kernel(last, *refs), out_shape=(jax.Shap...]
    unnamed x3 -> x7, local copies, waits for them, and re-layouts: 7.75 us -> 7.92 us
where the time goes in v3:
time: 360 us
  Pallas kernels  338 us (94%)
  local copies, waits for them, and re-layouts  20.8 us (6%)
    pallas_call x2, Pallas kernels, backward(): pl.pallas_call(lambda *refs: bwd_kernel(last, *refs), out_shape=(jax.Shap...  255 us
    pallas_call x1, Pallas kernels, forward(): pl.pallas_call(fwd_kernel, out_shape=(jax.ShapeDtypeStruct((NB, TB, D), b...  82.7 us
    unnamed x7, local copies, waits for them, and re-layouts  7.92 us

profile of v3, /device:TPU:0, one launch (start us, length us, event | category | flops | bytes accessed | tf_op | source)
XLA Modules:
  0.0 360.0 jit_solution(10939779934174534274)
XLA Ops:
  0.6 82.7 %forward_gather.1 = (bf16[8,512,640]{2,1,0:T(8,128)(2,1)}, bf16[2,4,4,2,80,512]{5,4,3,2,1,0:T(8,128)(2,1)}, bf16[4,4,2,64,640]{4,3,2,1,0:T(8,128)(2,1)}, bf16[2,...) custom-call(bf16[8,512,640]{2,1,0:T(8,128)(2,1)} %bitcast.23, ...), custom_call_target="tpu_custom_call" | custom-call | flops 32212254720 | bytes 20000000 | tf_op jit(solution)/shard_map/forward_gather/pallas_call | solution.py:258
  83.3 134.3 %backward_1.1 = (bf16[8,512,640]{2,1,0:T(8,128)(2,1)}, bf16[3,2,2,2,4,80,128]{6,5,4,3,2,1,0:T(8,128)(2,1)}, bf16[3,3,2,4,80,128]{5,4,3,2,1,0:T(8,128)(2,1)}) custom-call(bf16[8,512,640]{2,1,0:T(8,128)(2,1)} %get-tuple-element.15.refs_0_, bf16[8,512,640]{2,1,0:T(8,128)(2,1)} %bitcast.22, bf16[2,4,4,2,80,512]{5,4,3,2,1,0:T(8,128)(2,1)} %get-tuple-element.16.refs_2_, ...), custom_call_target="tpu_custom_call" | custom-call | flops 85899345920 | bytes 30000000 | tf_op jit(solution)/shard_map/backward_1/pallas_call | solution.py:606
  217.6 121.0 %backward_0.1 = (bf16[8,512,640]{2,1,0:T(8,128)(2,1)}, bf16[4,8,2,512,512]{4,3,2,1,0:T(8,128)(2,1)}, bf16[5,3,2,4,80,128]{5,4,3,2,1,0:T(8,128)(2,1)}) custom-call(bf16[8,512,640]{2,1,0:T(8,128)(2,1)} %bitcast.24, bf16[8,512,640]{2,1,0:T(8,128)(2,1)} %get-tuple-element.18.refs_1_, bf16[2,4,4,2,80,512]{5,4,3,2,1,0:T(8,128)(2,1)} %get-tuple-element.19.refs_2_, ...), custom_call_target="tpu_custom_call" | custom-call | flops 64424509440 | bytes 30000000 | tf_op jit(solution)/shard_map/backward_0/pallas_call | solution.py:606
  338.6 1.1 slice.16
  339.7 0.0 copy-start.1
  339.7 1.8 slice.15
  341.4 0.2 copy-done.1
  341.6 0.5 pad_maximum_fusion
  342.1 2.4 fusion
  344.6 1.0 copy.18
  345.6 0.5 reshape.35
  346.1 1.4 copy.15
  347.6 0.0 copy-start
  347.6 2.4 copy.13
  350.0 1.8 reshape.34
  351.8 0.0 copy-done
  351.8 1.0 copy.12
  352.9 1.8 reshape.33
  354.7 5.3 %copy.20 = bf16[1,4096,640]{2,1,0:T(8,128)(2,1)} copy(bf16[1,4096,640]{2,1,0:T(8,128)(2,1)} %bitcast.20) | data formatting | bytes 10485760
Async XLA Ops:
  339.7 2.0 copy-start.1
  347.6 4.3 %copy-start = (bf16[2,2,80,4,4,128]{5,2,3,1,4,0:T(8,128)(2,1)S(1)}, bf16[2,2,80,4,4,128]{5,2,3,1,4,0:T(8,128)(2,1)}, u32[]{:S(2)}) copy-start(bf16[2,2,80,4,4,128]{5,2,3,1,4,0:T(8,128)(2,1)} %get-tuple-element.32) | copy-start | bytes 3932164
